TPU v7x, 32 devices: a whole 2x2x4 slice. The times are simulated.
32 devices in a mesh: row: 8 (over y, x, core), col: 4 (over z).
Axes of the slice: x: 2, y: 2, z: 4, core: 2. Of those that a mesh axis runs over, the one named last changes fastest.
Arguments:
- history: float32 [3, 512, 4096], P(None, None, ('row', 'col')), may hold values from -8 to 8
Outputs:
- orbitals: float32 [512, 4096], P(None, ('row', 'col'))
All inputs are finite; a program needn't handle non-finite values.
Results may differ from a plain program's by a relative error of at most 0.0003.
Values sent between devices are 32-bit elements; how exact they have to be, the bound alone decides.
No kernel may reach another device: no remote copies, remote signals or barrier semaphores. Data moves between devices by JAX's collectives and lax.ppermute only.
A program may use at most 64 MiB of HBM per device.

v0:
```python
import functools

import jax
import jax.numpy as jnp
from jax import lax
from jax.experimental import pallas as pl
from jax.experimental.pallas import tpu as pltpu
from jax.sharding import PartitionSpec as P


HIGHEST = lax.Precision.HIGHEST
WEIGHTS = (2.5, -2.0, 0.5)
TILE = 128
PANEL = 32
GROUP = 16
AHEAD = 4
VMEM_LIMIT = 16 << 20
AXES = ("row", "col")
NT = (((1,), (1,)), ((), ()))
NN = (((1,), (0,)), ((), ()))
TN = (((0,), (0,)), ((), ()))


def dot(a, b, dims):
    return lax.dot_general(a, b, dims, precision=HIGHEST, preferred_element_type=jnp.float32)


def bf16_dot(a, b, dims):
    return lax.dot_general(a, b, dims, preferred_element_type=jnp.float32)


def split(x):
    high = x.astype(jnp.bfloat16)
    rest = x - high.astype(jnp.float32)
    middle = rest.astype(jnp.bfloat16)
    return high, middle, (rest - middle.astype(jnp.float32)).astype(jnp.bfloat16)


def stacked(x, axis):
    h, m, low = split(x)
    return jnp.concatenate([h, h, m, h, low, m], axis=axis), jnp.concatenate([h, m, h, low, h, m], axis=axis)


class Route:
    def __init__(self, mesh_rows, mesh_cols):
        self.rows, self.cols = mesh_rows, mesh_cols
        row_bits = list(range(1, mesh_rows.bit_length() - 1))
        col_bits = list(range(mesh_cols.bit_length() - 1))
        half = len(row_bits) // 2
        orders = (row_bits, row_bits[half:] + row_bits[:half])
        self.row_levels = len(row_bits)
        self.orders = tuple(
            [("row", b) for b in order] + [("col", b) for b in col_bits] for order in orders
        )
        self.levels = len(self.orders[0])

    def scatter(self, norb):
        return min(self.levels, (norb // 16).bit_length() - 1)

    def core(self):
        return lax.axis_index("row") & 1

    def core_perm(self):
        c = self.cols
        return [(r * c + k, (r ^ 1) * c + k) for r in range(self.rows) for k in range(c)]

    def perm(self, *levels):
        pairs = []
        for r in range(self.rows):
            for k in range(self.cols):
                flip = {"row": 0, "col": 0}
                for level in levels:
                    axis, bit = self.orders[r & 1][level]
                    flip[axis] ^= 1 << bit
                pairs.append((r * self.cols + k, (r ^ flip["row"]) * self.cols + (k ^ flip["col"])))
        return pairs

    def perms(self, first, count):
        return [
            self.perm(*[first + i for i in range(count) if q >> (count - 1 - i) & 1]) for q in range(1, 1 << count)
        ]

    def place(self, core, levels):
        index = {"row": lax.axis_index("row"), "col": lax.axis_index("col")}
        numbers = []
        for order in self.orders:
            number = jnp.int32(0)
            for axis, bit in order[:levels]:
                number = number * 2 + ((index[axis] >> bit) & 1)
            numbers.append(number)
        return jnp.where(core == 0, numbers[0], numbers[1])


def swap(x, perm):
    return lax.ppermute(x, AXES, perm)


def all_reduce(route, keep, send, scatter, levels):
    def step(x, level):
        return swap(x, route.perm(level))

    for level in range(scatter):
        got = step(send, level)
        if level < scatter - 1:
            half = keep.shape[0] // 2
            keep, send = keep[:half] + got[:half], keep[half:] + got[half:]
        else:
            keep = lax.optimization_barrier(keep + got)
    for level in range(scatter, levels):
        keep = keep + step(keep, level)
    for level in reversed(range(scatter)):
        keep = jnp.concatenate([keep, step(keep, level)], axis=0)
    return keep


def phases(first, last):
    return [(level, min(2, last - level)) for level in range(first, last, 2)]


def direct_all_reduce(route, pieces, scatter, levels):
    for number, (level, count) in enumerate(phases(0, scatter)):
        if number > 0:
            size = keep.shape[0] >> count
            pieces = [keep[q * size : (q + 1) * size] for q in range(1 << count)]
        got = [swap(piece, perm) for piece, perm in zip(pieces[1:], route.perms(level, count))]
        keep = functools.reduce(jnp.add, got, pieces[0])
    for level, count in phases(scatter, levels):
        keep = functools.reduce(jnp.add, [swap(keep, perm) for perm in route.perms(level, count)], keep)
    for level, count in reversed(phases(0, scatter)):
        keep = jnp.concatenate([keep] + [swap(keep, perm) for perm in route.perms(level, count)])
    return keep


def fetch_kernel(in_ref, out_ref):
    pltpu.sync_copy(in_ref, out_ref)


def project_kernel(j, left_ref, own_ref, peer_ref, keep_ref, send_ref):
    half = keep_ref.shape[0]
    right = stacked(jnp.concatenate([own_ref[j], peer_ref[j]], axis=1), axis=1)[1]
    keep_ref[...] = bf16_dot(left_ref[:half, :], right, NT)
    send_ref[...] = bf16_dot(left_ref[half:, :], right, NT)


def first_project_kernel(route, scatter, own_ref, peer_ref, keep_ref, send_ref, left_ref, left, right):
    rows, width, blocks, quarter = left.shape[0], own_ref.shape[2], 1 << scatter, keep_ref.shape[0]
    core = route.core()
    place = route.place(core, scatter)
    size = rows // blocks
    for k in range(blocks):
        at = pl.multiple_of(core * rows + (place ^ k) * size, size)
        left[k * size : (k + 1) * size, :width] = own_ref[0, pl.ds(at, size), :]
        left[k * size : (k + 1) * size, width:] = peer_ref[0, pl.ds(at, size), :]
    left_ref[...] = stacked(left[...], axis=1)[0]
    right[...] = stacked(jnp.concatenate([own_ref[0], peer_ref[0]], axis=1), axis=1)[1]
    top = place >> (scatter - 1)
    for g, ref in enumerate((keep_ref, send_ref)):
        number = 2 * core + (g ^ top)
        for t in range(3):
            at = pl.multiple_of(((number + t) & 3) * quarter, quarter)
            ref[:, t * quarter : (t + 1) * quarter] = bf16_dot(
                left_ref[g * quarter : (g + 1) * quarter, :], right[pl.ds(at, quarter), :], NT
            )


def lend_kernel(route, scatter, m_ref, out_ref):
    half_blocks, quarter = 1 << (scatter - 1), out_ref.shape[0]
    place, size = route.place(route.core(), scatter), quarter // half_blocks
    for k in range(half_blocks):
        at = pl.multiple_of((place ^ (half_blocks + k)) * size, size)
        out_ref[k * size : (k + 1) * size, :] = m_ref[pl.ds(at, size), quarter : 2 * quarter]


def first_predict_kernel(scale, route, scatter, m_ref, lent_ref, own_ref, peer_ref, out_ref, x, block, turned, full):
    half_blocks, quarter, width = 1 << (scatter - 1), lent_ref.shape[0], own_ref.shape[2]
    core = route.core()
    place = route.place(core, scatter)
    top, low = place >> (scatter - 1), place & (half_blocks - 1)
    size = quarter // half_blocks
    x[:, :width] = own_ref[0]
    x[:, width:] = peer_ref[0]
    for k in range(half_blocks):
        at = pl.multiple_of((place ^ k) * size, size)
        block[k * size : (k + 1) * size, :] = m_ref[pl.ds(at, size), quarter : 2 * quarter]
    turned[0] = jnp.transpose(lent_ref[...])
    turned[1] = jnp.transpose(block[...])
    for g in range(2):
        number = 2 * core + (g ^ top)
        full[:, : 3 * quarter] = m_ref[g * quarter : (g + 1) * quarter, :]
        for k in range(half_blocks):
            at = pl.multiple_of((k ^ low) * size, size)
            full[k * size : (k + 1) * size, 3 * quarter :] = turned[g ^ top, pl.ds(at, size), :]
        parts = [x[pl.ds(pl.multiple_of(((number + t) & 3) * quarter, quarter), quarter), :] for t in range(4)]
        right = stacked(jnp.concatenate(parts, axis=0), axis=0)[1]
        out_ref[g * quarter : (g + 1) * quarter, :] = bf16_dot(stacked(full[...], axis=1)[0], right, NN) * scale


def term(j, scale, m_ref, own_ref, peer_ref):
    left = stacked(m_ref[...], axis=1)[0]
    right = stacked(jnp.concatenate([own_ref[j], peer_ref[j]], axis=1), axis=0)[1]
    return bf16_dot(left, right, NN) * scale


def predict_kernel(j, scale, m_ref, own_ref, peer_ref, *refs):
    value = term(j, scale, m_ref, own_ref, peer_ref)
    refs[-1][...] = value + refs[0][...] if len(refs) > 1 else value


def last_predict_kernel(j, scale, route, scatter, m_ref, own_ref, peer_ref, sum_ref, out_ref, total):
    total[...] = term(j, scale, m_ref, own_ref, peer_ref) + sum_ref[...]
    place, blocks = route.place(route.core(), scatter), 1 << scatter
    size = total.shape[0] // blocks
    for k in range(blocks):
        out_ref[pl.ds(pl.multiple_of((place ^ k) * size, size), size), :] = total[k * size : (k + 1) * size, :]


def core_blocks(count):
    blocks = [(i, j) for i in range(count) for j in range(i, count)]
    half = (len(blocks) + 1) // 2
    return blocks[:half], blocks[half:]


def gram_kernel(route, scale, mine_ref, other_ref, *refs):
    outs, own_ref, p, acc = refs[:-3], refs[-3], refs[-2], refs[-1]
    half, width = mine_ref.shape[0], own_ref.shape[1]
    count = 2 * half // TILE
    lists = core_blocks(count)
    parts, core = 1 << route.row_levels, route.core()
    place = route.place(core, route.row_levels)
    here = pl.ds(pl.multiple_of(core * half, half), half)
    there = pl.ds(pl.multiple_of((1 - core) * half, half), half)
    p[here, :] = mine_ref[...]
    p[there, :width] = other_ref[:, width:]
    p[there, width:] = other_ref[:, :width]
    own_ref[...] = p[:, :width]
    for n in range(len(lists[0])):
        first = lists[0][n]
        second = lists[1][min(n, len(lists[1]) - 1)]
        i = jnp.where(core == 0, first[0], second[0])
        j = jnp.where(core == 0, first[1], second[1])
        a = p[pl.ds(pl.multiple_of(i * TILE, TILE), TILE), :]
        b = p[pl.ds(pl.multiple_of(j * TILE, TILE), TILE), :]
        acc[n * TILE : (n + 1) * TILE, :] = dot(a, b, NT) * scale
    size = acc.shape[0] // parts
    for k in range(parts):
        each = parts // len(outs)
        outs[k // each][k % each * size : (k % each + 1) * size, :] = acc[pl.ds(pl.multiple_of((place ^ k) * size, 8), size), :]


def solve_kernel(route, mine_ref, other_ref, p_ref, out_ref, natural, work, stack_a, stack_b):
    n, tile = p_ref.shape[0], TILE
    width = n + p_ref.shape[1]
    count, groups, per_panel, panels = n // tile, width // tile, PANEL // 8, tile // PANEL
    parts, core = 1 << route.row_levels, route.core()
    size = mine_ref.shape[0] // parts
    for ref, number in ((mine_ref, core), (other_ref, 1 - core)):
        place = route.place(number, route.row_levels)
        for k in range(parts):
            at = pl.multiple_of((place ^ k) * size, 8)
            natural[number, pl.ds(at, size), :] = ref[k * size : (k + 1) * size, :]
    for number, blocks in enumerate(core_blocks(count)):
        for at, (i, j) in enumerate(blocks):
            work[i * tile : (i + 1) * tile, j * tile : (j + 1) * tile] = natural[number, at * tile : (at + 1) * tile, :]
    work[:, n:] = p_ref[...]
    sub = lax.broadcasted_iota(jnp.int32, (8, tile), 0)
    deep = 6 * PANEL

    def panel(b, s):
        base = b * tile + PANEL * s
        r = [
            [work[base + 8 * i : base + 8 * i + 8, c * tile : (c + 1) * tile] for c in range(b, groups)]
            for i in range(per_panel)
        ]
        scale = [jnp.zeros((8, tile), jnp.float32)] * per_panel
        cols = {}
        for j in range(PANEL):
            start = 0 if j == 0 else j + AHEAD
            if start % GROUP == 0 and start < PANEL:
                for k in range(start, start + GROUP):
                    at = PANEL * s + k
                    cols[k] = {i: jnp.broadcast_to(r[i][0][:, at : at + 1], (8, tile)) for i in range(k // 8, per_panel)}
            jb, js = j // 8, j % 8
            col = cols[j]
            pivot = jnp.broadcast_to(col[jb][js : js + 1, :], (8, tile)) if j == 0 else following
            scale[jb] = jnp.where(sub == js, lax.rsqrt(pivot), scale[jb])
            inverse = 1.0 / pivot
            below = {i: col[i] if i > jb else jnp.where(sub > js, col[i], 0.0) for i in range(jb, per_panel)}
            mult = {i: below[i] * inverse for i in range(jb, per_panel)}
            first = jb if js < 7 else jb + 1
            for k in range(j + 1, len(cols)):
                row = jnp.broadcast_to(col[k // 8][k % 8 : k % 8 + 1, :], (8, tile))
                if k == j + 1:
                    following = jnp.broadcast_to(cols[k][k // 8][k % 8 : k % 8 + 1, :], (8, tile)) - row * row * inverse
                for i in range(k // 8, per_panel):
                    cols[k][i] = cols[k][i] - mult[i] * row
            for c in range(groups - b):
                row = jnp.broadcast_to(r[jb][c][js : js + 1, :], (8, tile))
                for i in range(first, per_panel):
                    r[i][c] = r[i][c] - mult[i] * row
        return jnp.concatenate(
            [jnp.concatenate([x * scale[i] for x in r[i]], axis=1) for i in range(per_panel)], axis=0
        )

    for b in range(count):
        start = b * tile
        for s in range(panels):
            u = panel(b, s)
            out_ref[start + PANEL * s : start + PANEL * (s + 1), :] = u[:, n - start :]
            if b == count - 1 and s == panels - 1:
                break
            left, right = stacked(u, axis=0)
            if s < panels - 1:
                flipped = jnp.transpose(left[:, :tile])
                low, high, near = PANEL * (s + 1), PANEL * (s + 2), min(start + 2 * tile, width)
                for rows, columns in (((low, high), (start, near)), ((low, high), (near, width)), ((high, tile), (start, width))):
                    if rows[0] < rows[1] and columns[0] < columns[1]:
                        work[start + rows[0] : start + rows[1], columns[0] : columns[1]] -= bf16_dot(
                            flipped[rows[0] : rows[1], :], right[:, columns[0] - start : columns[1] - start], NN
                        )
            if b < count - 1:
                stack_a[deep * s : deep * (s + 1), start:n] = left[:, : n - start]
                stack_b[deep * s : deep * (s + 1), start:] = right
        for i in range(b + 1, count):
            at = i * tile
            work[at : at + tile, at:] -= bf16_dot(stack_a[:, at : at + tile], stack_b[:, at:], TN)


VMEM = pl.BlockSpec(memory_space=pltpu.VMEM)


def f32(*shape):
    return jax.ShapeDtypeStruct(shape, jnp.float32)


def call(kernel, out_shape, scratch, args, flops=0):
    moved = sum(x.size * x.dtype.itemsize for x in list(args) + jax.tree.leaves(out_shape))
    return pl.pallas_call(
        kernel,
        cost_estimate=pl.CostEstimate(flops=flops, bytes_accessed=moved, transcendentals=0),
        out_shape=out_shape,
        in_specs=[VMEM] * len(args),
        out_specs=jax.tree.map(lambda _: VMEM, out_shape),
        scratch_shapes=[pltpu.VMEM(s.shape, s.dtype) for s in scratch],
        compiler_params=pltpu.CompilerParams(vmem_limit_bytes=VMEM_LIMIT),
    )(*args)


def on_device(rows, cols, history):
    return orbitals(rows, cols, history)


def orbitals(rows, cols, history):
    route = Route(rows, cols)
    terms, norb, width = history.shape
    total = width * rows * cols
    half = norb // 2

    levels, scatter = route.levels, route.scatter(norb)

    peer = swap(history, route.core_perm())
    own = pl.pallas_call(
        fetch_kernel,
        name="fetch",
        out_shape=f32(*history.shape),
        in_specs=[pl.BlockSpec(memory_space=pl.ANY)],
        out_specs=VMEM,
        compiler_params=pltpu.CompilerParams(vmem_limit_bytes=VMEM_LIMIT),
    )(history)
    flops = 6 * 2 * half * norb * 2 * width
    out, quarter = [f32(half // 2, norb)] * 2, norb // 4
    keep, send, left = call(
        functools.partial(first_project_kernel, route, scatter),
        [f32(quarter, 3 * quarter)] * 2 + [jax.ShapeDtypeStruct((half, 12 * width), jnp.bfloat16)],
        [f32(half, 2 * width), jax.ShapeDtypeStruct((norb, 12 * width), jnp.bfloat16)],
        [own, peer],
        flops=flops,
    )
    products = [(keep, send)]
    for j in range(1, terms):
        products.append(call(functools.partial(project_kernel, j), out, [], [left, own, peer], flops))
    m = [all_reduce(route, keep, send, scatter, levels) for keep, send in products]
    out = f32(half, 2 * width)
    lent = call(functools.partial(lend_kernel, route, scatter), f32(quarter, quarter), [], [m[0]])
    lent = swap(lent, route.core_perm())
    kernel = functools.partial(first_predict_kernel, WEIGHTS[0] / total, route, scatter)
    scratch = [f32(norb, 2 * width), f32(quarter, quarter), f32(2, quarter, quarter), f32(quarter, norb)]
    mine = [call(kernel, out, scratch, [m[0], lent, own, peer], flops)]
    for j in range(1, terms - 1):
        kernel = functools.partial(predict_kernel, j, WEIGHTS[j] / total)
        mine = [call(kernel, out, [], [m[j], own, peer] + mine, flops)]
    kernel = functools.partial(last_predict_kernel, terms - 1, WEIGHTS[terms - 1] / total, route, scatter)
    mine = call(kernel, out, [out], [m[-1], own, peer] + mine, flops)
    other = swap(mine, route.core_perm())

    shares = (norb // TILE) * (norb // TILE + 1) // 2
    share = (shares + 1) // 2 * TILE
    ways = 1 << min(2, route.row_levels)
    *pieces, predicted = call(
        functools.partial(gram_kernel, route, 1.0 / total),
        [f32(share // ways, TILE)] * ways + [f32(norb, width)],
        [f32(norb, 2 * width), f32(share, TILE)],
        [mine, other],
    )
    gram = direct_all_reduce(route, pieces, route.row_levels, levels)
    gram_other = swap(gram, route.core_perm())
    return call(
        functools.partial(solve_kernel, route),
        f32(norb, width),
        [
            f32(2, share, TILE),
            f32(norb, norb + width),
            jax.ShapeDtypeStruct((6 * TILE, norb), jnp.bfloat16),
            jax.ShapeDtypeStruct((6 * TILE, norb + width), jnp.bfloat16),
        ],
        [gram, gram_other, predicted],
    )


def solution(mesh):
    rows, cols = mesh.shape["row"], mesh.shape["col"]

    def program(history):
        step = jax.shard_map(
            functools.partial(on_device, rows, cols),
            mesh=mesh,
            in_specs=(P(None, None, AXES),),
            out_specs=P(None, AXES),
            check_vma=False,
        )
        return step(history)

    return program
```

profile of v0, /device:TPU:0, one launch (start us, length us, event | category | flops | bytes accessed | tf_op | source)
XLA Modules:
  0.0 110.6 jit_solution(94624557746669145)
XLA Ops:
  3.6 2.9 %collective-permute-start.17 = (f32[128,384]{1,0:T(8,128)S(1)}, f32[128,384]{1,0:T(8,128)S(1)}, u32[]{:S(2)}, u32[]{:S(2)}) collective-permute-start(f32[128,384]{1,0:T(8,128)S(1)} %get-tuple-element.23), channel_id=1, source_target_pairs={{0,8},{1,9},{2,10},{3,11},{4,20},{5,21},{6,22},{7,23},{8,0},{9,1},... | collective-permute-start | bytes 589832 | tf_op jit(solution)/shard_map/ppermute | solution.py:95
  6.5 3.6 %collective-permute-done.17 = f32[128,384]{1,0:T(8,128)S(1)} collective-permute-done((f32[128,384]{1,0:T(8,128)S(1)}, f32[128,384]{1,0:T(8,128)S(1)}, u32[]{:S(2)}, u32[]{:S(2)}) %collective-permute-start.17) | collective-permute-done | bytes 196640 | tf_op jit(solution)/shard_map/ppermute | solution.py:95
  10.2 2.1 %collective-permute-start.18 = (f32[64,384]{1,0:T(8,128)S(1)}, f32[64,384]{1,0:T(8,128)S(1)}, u32[]{:S(2)}, u32[]{:S(2)}) collective-permute-start(f32[64,384]{1,0:T(8,128)S(1)} %get-tuple-element.34), channel_id=1, source_target_pairs={{0,16},{1,17},{2,18},{3,19},{4,12},{5,13},{6,14},{7,15},{8,24},{9,... | collective-permute-start | bytes 294920 | tf_op jit(solution)/shard_map/ppermute | solution.py:95
  16.8 1.6 %collective-permute-start.19 = (f32[32,384]{1,0:T(8,128)S(1)}, f32[32,384]{1,0:T(8,128)S(1)}, u32[]{:S(2)}, u32[]{:S(2)}) collective-permute-start(f32[32,384]{1,0:T(8,128)S(1)} %get-tuple-element.40), channel_id=1, source_target_pairs={{0,1},{1,0},{2,3},{3,2},{4,5},{5,4},{6,7},{7,6},{8,9},{9,8},{10,11... | collective-permute-start | bytes 147464 | tf_op jit(solution)/shard_map/ppermute | solution.py:95
  20.9 2.6 %collective-permute-start.20 = (f32[16,384]{1,0:T(8,128)S(1)}, f32[16,384]{1,0:T(8,128)S(1)}, u32[]{:S(2)}, u32[]{:S(2)}) collective-permute-start(f32[16,384]{1,0:T(8,128)S(1)} %slice_add_fusion.16), channel_id=1, source_target_pairs={{0,2},{1,3},{2,0},{3,1},{4,6},{5,7},{6,4},{7,5},{8,10},{9,11},{10,... | collective-permute-start | bytes 73736 | tf_op jit(solution)/shard_map/ppermute | solution.py:95
  25.7 2.6 %collective-permute-start.21 = (f32[16,384]{1,0:T(8,128)S(1)}, f32[16,384]{1,0:T(8,128)S(1)}, u32[]{:S(2)}, u32[]{:S(2)}) collective-permute-start(f32[16,384]{1,0:T(8,128)S(1)} %fusion.2), channel_id=1, source_target_pairs={{0,2},{1,3},{2,0},{3,1},{4,6},{5,7},{6,4},{7,5},{8,10},{9,11},{10,... | collective-permute-start | bytes 73736 | tf_op jit(solution)/shard_map/ppermute | solution.py:95
  28.3 1.8 %collective-permute-start.11 = (f32[32,512]{1,0:T(8,128)S(1)}, f32[32,512]{1,0:T(8,128)S(1)}, u32[]{:S(2)}, u32[]{:S(2)}) collective-permute-start(f32[32,512]{1,0:T(8,128)S(1)} %get-tuple-element.36), channel_id=1, source_target_pairs={{0,1},{1,0},{2,3},{3,2},{4,5},{5,4},{6,7},{7,6},{8,9},{9,8},{10,11... | collective-permute-start | bytes 196616 | tf_op jit(solution)/shard_map/ppermute | solution.py:95
  32.3 2.7 %collective-permute-done.22 = f32[32,384]{1,0:T(8,128)S(1)} collective-permute-done((f32[32,384]{1,0:T(8,128)S(1)}, f32[32,384]{1,0:T(8,128)S(1)}, u32[]{:S(2)}, u32[]{:S(2)}) %collective-permute-start.22) | collective-permute-done | bytes 49184 | tf_op jit(solution)/shard_map/ppermute | solution.py:95
  36.2 2.5 %collective-permute-start.4 = (f32[16,512]{1,0:T(8,128)S(1)}, f32[16,512]{1,0:T(8,128)S(1)}, u32[]{:S(2)}, u32[]{:S(2)}) collective-permute-start(f32[16,512]{1,0:T(8,128)S(1)} %slice_add_fusion.14), channel_id=1, source_target_pairs={{0,2},{1,3},{2,0},{3,1},{4,6},{5,7},{6,4},{7,5},{8,10},{9,11},{10,... | collective-permute-start | bytes 98312 | tf_op jit(solution)/shard_map/ppermute | solution.py:95
  39.3 1.8 %collective-permute-done.4 = f32[16,512]{1,0:T(8,128)S(1)} collective-permute-done((f32[16,512]{1,0:T(8,128)S(1)}, f32[16,512]{1,0:T(8,128)S(1)}, u32[]{:S(2)}, u32[]{:S(2)}) %collective-permute-start.4) | collective-permute-done | bytes 32800 | tf_op jit(solution)/shard_map/ppermute | solution.py:95
  41.1 2.5 %collective-permute-start.5 = (f32[16,512]{1,0:T(8,128)S(1)}, f32[16,512]{1,0:T(8,128)S(1)}, u32[]{:S(2)}, u32[]{:S(2)}) collective-permute-start(f32[16,512]{1,0:T(8,128)S(1)} %fusion.1), channel_id=1, source_target_pairs={{0,2},{1,3},{2,0},{3,1},{4,6},{5,7},{6,4},{7,5},{8,10},{9,11},{10,... | collective-permute-start | bytes 98312 | tf_op jit(solution)/shard_map/ppermute | solution.py:95
  44.2 4.3 %collective-permute-done.13 = f32[16,512]{1,0:T(8,128)S(1)} collective-permute-done((f32[16,512]{1,0:T(8,128)S(1)}, f32[16,512]{1,0:T(8,128)S(1)}, u32[]{:S(2)}, u32[]{:S(2)}) %collective-permute-start.13) | collective-permute-done | bytes 32800 | tf_op jit(solution)/shard_map/ppermute | solution.py:95
  48.5 2.2 %collective-permute-start.14 = (f32[32,512]{1,0:T(8,128)S(1)}, f32[32,512]{1,0:T(8,128)S(1)}, u32[]{:S(2)}, u32[]{:S(2)}) collective-permute-start(f32[32,512]{1,0:T(8,128)S(1)} %pad_maximum_fusion.8), channel_id=1, source_target_pairs={{0,1},{1,0},{2,3},{3,2},{4,5},{5,4},{6,7},{7,6},{8,9},{9,8},{10,11... | collective-permute-start | bytes 196616 | tf_op jit(solution)/shard_map/ppermute | solution.py:95
  50.8 1.7 %collective-permute-start.24 = (f32[128,384]{1,0:T(8,128)S(1)}, f32[128,384]{1,0:T(8,128)S(1)}, u32[]{:S(2)}, u32[]{:S(2)}) collective-permute-start(f32[128,384]{1,0:T(8,128)S(1)} %pad_maximum_fusion.3), channel_id=1, source_target_pairs={{0,8},{1,9},{2,10},{3,11},{4,20},{5,21},{6,22},{7,23},{8,0},{9,1},... | collective-permute-start | bytes 589832 | tf_op jit(solution)/shard_map/ppermute | solution.py:95
  56.5 2.8 %collective-permute-done.15 = f32[64,512]{1,0:T(8,128)S(1)} collective-permute-done((f32[64,512]{1,0:T(8,128)S(1)}, f32[64,512]{1,0:T(8,128)S(1)}, u32[]{:S(2)}, u32[]{:S(2)}) %collective-permute-start.15) | collective-permute-done | bytes 131104 | tf_op jit(solution)/shard_map/ppermute | solution.py:95
  63.9 4.7 %collective-permute-done.8 = f32[128,512]{1,0:T(8,128)S(1)} collective-permute-done((f32[128,512]{1,0:T(8,128)S(1)}, f32[128,512]{1,0:T(8,128)S(1)}, u32[]{:S(2)}, u32[]{:S(2)}) %collective-permute-start.8) | collective-permute-done | bytes 262176 | tf_op jit(solution)/shard_map/ppermute | solution.py:95
  78.2 1.8 %collective-permute-done.29 = f32[160,128]{1,0:T(8,128)S(1)} collective-permute-done((f32[160,128]{1,0:T(8,128)S(1)}, f32[160,128]{1,0:T(8,128)S(1)}, u32[]{:S(2)}, u32[]{:S(2)}) %collective-permute-start.29) | collective-permute-done | bytes 81952 | tf_op jit(solution)/shard_map/ppermute | solution.py:95
  80.0 1.6 %collective-permute-start.32 = (f32[160,128]{1,0:T(8,128)S(1)}, f32[160,128]{1,0:T(8,128)S(1)}, u32[]{:S(2)}, u32[]{:S(2)}) collective-permute-start(f32[160,128]{1,0:T(8,128)S(1)} %add_add_fusion.1), channel_id=1, source_target_pairs={{0,3},{1,2},{2,1},{3,0},{4,7},{5,6},{6,5},{7,4},{8,11},{9,10},{10,... | collective-permute-start | bytes 245768 | tf_op jit(solution)/shard_map/ppermute | solution.py:95
  81.6 2.8 %collective-permute-start.30 = (f32[160,128]{1,0:T(8,128)S(1)}, f32[160,128]{1,0:T(8,128)S(1)}, u32[]{:S(2)}, u32[]{:S(2)}) collective-permute-start(f32[160,128]{1,0:T(8,128)S(1)} %add_add_fusion.1), channel_id=1, source_target_pairs={{0,2},{1,3},{2,0},{3,1},{4,6},{5,7},{6,4},{7,5},{8,10},{9,11},{10,... | collective-permute-start | bytes 245768 | tf_op jit(solution)/shard_map/ppermute | solution.py:95
  84.4 2.8 %collective-permute-done.32 = f32[160,128]{1,0:T(8,128)S(1)} collective-permute-done((f32[160,128]{1,0:T(8,128)S(1)}, f32[160,128]{1,0:T(8,128)S(1)}, u32[]{:S(2)}, u32[]{:S(2)}) %collective-permute-start.32) | collective-permute-done | bytes 81952 | tf_op jit(solution)/shard_map/ppermute | solution.py:95
  87.3 2.6 %collective-permute-done.30 = f32[160,128]{1,0:T(8,128)S(1)} collective-permute-done((f32[160,128]{1,0:T(8,128)S(1)}, f32[160,128]{1,0:T(8,128)S(1)}, u32[]{:S(2)}, u32[]{:S(2)}) %collective-permute-start.30) | collective-permute-done | bytes 81952 | tf_op jit(solution)/shard_map/ppermute | solution.py:95
  93.4 1.9 %collective-permute-done.35 = f32[160,128]{1,0:T(8,128)S(1)} collective-permute-done((f32[160,128]{1,0:T(8,128)S(1)}, f32[160,128]{1,0:T(8,128)S(1)}, u32[]{:S(2)}, u32[]{:S(2)}) %collective-permute-start.35) | collective-permute-done | bytes 81952 | tf_op jit(solution)/shard_map/ppermute | solution.py:95
  96.7 1.6 %collective-permute-done.36.other_ref = f32[640,128]{1,0:T(8,128)S(1)} collective-permute-done((f32[640,128]{1,0:T(8,128)S(1)}, f32[640,128]{1,0:T(8,128)S(1)}, u32[]{:S(2)}, u32[]{:S(2)}) %collective-permute-start.36) | collective-permute-done | bytes 327712 | tf_op jit(solution)/shard_map/ppermute | solution.py:95
  98.3 12.3 %shard_map.25 = f32[512,128]{1,0:T(8,128)} custom-call(f32[640,128]{1,0:T(8,128)S(1)} %pad_maximum_fusion.mine_ref, f32[640,128]{1,0:T(8,128)S(1)} %collective-permute-done.36.other_ref, f32[512,128]{1,0:T(8,128)S(1)} %get-tuple-element.28.p_ref), custom_call_target="tpu_custom_call" | custom-call | bytes 1179648 | tf_op jit(solution)/shard_map/pallas_call | solution.py:337
  (101 shorter events, 40.5 us)
Async XLA Ops:
  3.6 6.6 %collective-permute-start.17 = (f32[128,384]{1,0:T(8,128)S(1)}, f32[128,384]{1,0:T(8,128)S(1)}, u32[]{:S(2)}, u32[]{:S(2)}) collective-permute-start(f32[128,384]{1,0:T(8,128)S(1)} %get-tuple-element.23), channel_id=1, source_target_pairs={{0,8},{1,9},{2,10},{3,11},{4,20},{5,21},{6,22},{7,23},{8,0},{9,1},... | collective-permute-start | bytes 589832 | tf_op jit(solution)/shard_map/ppermute | solution.py:95
  10.2 6.6 %collective-permute-start.18 = (f32[64,384]{1,0:T(8,128)S(1)}, f32[64,384]{1,0:T(8,128)S(1)}, u32[]{:S(2)}, u32[]{:S(2)}) collective-permute-start(f32[64,384]{1,0:T(8,128)S(1)} %get-tuple-element.34), channel_id=1, source_target_pairs={{0,16},{1,17},{2,18},{3,19},{4,12},{5,13},{6,14},{7,15},{8,24},{9,... | collective-permute-start | bytes 294920 | tf_op jit(solution)/shard_map/ppermute | solution.py:95
  13.4 6.4 %collective-permute-start.9 = (f32[128,512]{1,0:T(8,128)S(1)}, f32[128,512]{1,0:T(8,128)S(1)}, u32[]{:S(2)}, u32[]{:S(2)}) collective-permute-start(f32[128,512]{1,0:T(8,128)S(1)} %get-tuple-element.21), channel_id=1, source_target_pairs={{0,8},{1,9},{2,10},{3,11},{4,20},{5,21},{6,22},{7,23},{8,0},{9,1},... | collective-permute-start | bytes 786440 | tf_op jit(solution)/shard_map/ppermute | solution.py:95
  16.1 7.9 %collective-permute-start.1 = (f32[128,512]{1,0:T(8,128)S(1)}, f32[128,512]{1,0:T(8,128)S(1)}, u32[]{:S(2)}, u32[]{:S(2)}) collective-permute-start(f32[128,512]{1,0:T(8,128)S(1)} %get-tuple-element.19), channel_id=1, source_target_pairs={{0,8},{1,9},{2,10},{3,11},{4,20},{5,21},{6,22},{7,23},{8,0},{9,1},... | collective-permute-start | bytes 786440 | tf_op jit(solution)/shard_map/ppermute | solution.py:95
  19.9 8.4 %collective-permute-start.10 = (f32[64,512]{1,0:T(8,128)S(1)}, f32[64,512]{1,0:T(8,128)S(1)}, u32[]{:S(2)}, u32[]{:S(2)}) collective-permute-start(f32[64,512]{1,0:T(8,128)S(1)} %get-tuple-element.30), channel_id=1, source_target_pairs={{0,16},{1,17},{2,18},{3,19},{4,12},{5,13},{6,14},{7,15},{8,24},{9,... | collective-permute-start | bytes 393224 | tf_op jit(solution)/shard_map/ppermute | solution.py:95
  24.1 5.9 %collective-permute-start.2 = (f32[64,512]{1,0:T(8,128)S(1)}, f32[64,512]{1,0:T(8,128)S(1)}, u32[]{:S(2)}, u32[]{:S(2)}) collective-permute-start(f32[64,512]{1,0:T(8,128)S(1)} %get-tuple-element.32), channel_id=1, source_target_pairs={{0,16},{1,17},{2,18},{3,19},{4,12},{5,13},{6,14},{7,15},{8,24},{9,... | collective-permute-start | bytes 393224 | tf_op jit(solution)/shard_map/ppermute | solution.py:95
  25.7 5.2 %collective-permute-start.21 = (f32[16,384]{1,0:T(8,128)S(1)}, f32[16,384]{1,0:T(8,128)S(1)}, u32[]{:S(2)}, u32[]{:S(2)}) collective-permute-start(f32[16,384]{1,0:T(8,128)S(1)} %fusion.2), channel_id=1, source_target_pairs={{0,2},{1,3},{2,0},{3,1},{4,6},{5,7},{6,4},{7,5},{8,10},{9,11},{10,... | collective-permute-start | bytes 73736 | tf_op jit(solution)/shard_map/ppermute | solution.py:95
  28.3 10.4 %collective-permute-start.11 = (f32[32,512]{1,0:T(8,128)S(1)}, f32[32,512]{1,0:T(8,128)S(1)}, u32[]{:S(2)}, u32[]{:S(2)}) collective-permute-start(f32[32,512]{1,0:T(8,128)S(1)} %get-tuple-element.36), channel_id=1, source_target_pairs={{0,1},{1,0},{2,3},{3,2},{4,5},{5,4},{6,7},{7,6},{8,9},{9,8},{10,11... | collective-permute-start | bytes 196616 | tf_op jit(solution)/shard_map/ppermute | solution.py:95
  30.1 6.1 %collective-permute-start.3 = (f32[32,512]{1,0:T(8,128)S(1)}, f32[32,512]{1,0:T(8,128)S(1)}, u32[]{:S(2)}, u32[]{:S(2)}) collective-permute-start(f32[32,512]{1,0:T(8,128)S(1)} %get-tuple-element.38), channel_id=1, source_target_pairs={{0,1},{1,0},{2,3},{3,2},{4,5},{5,4},{6,7},{7,6},{8,9},{9,8},{10,11... | collective-permute-start | bytes 196616 | tf_op jit(solution)/shard_map/ppermute | solution.py:95
  35.0 15.8 %collective-permute-start.23 = (f32[64,384]{1,0:T(8,128)S(1)}, f32[64,384]{1,0:T(8,128)S(1)}, u32[]{:S(2)}, u32[]{:S(2)}) collective-permute-start(f32[64,384]{1,0:T(8,128)S(1)} %pad_maximum_fusion.6), channel_id=1, source_target_pairs={{0,16},{1,17},{2,18},{3,19},{4,12},{5,13},{6,14},{7,15},{8,24},{9,... | collective-permute-start | bytes 294920 | tf_op jit(solution)/shard_map/ppermute | solution.py:95
  38.7 4.9 %collective-permute-start.12 = (f32[16,512]{1,0:T(8,128)S(1)}, f32[16,512]{1,0:T(8,128)S(1)}, u32[]{:S(2)}, u32[]{:S(2)}) collective-permute-start(f32[16,512]{1,0:T(8,128)S(1)} %slice_add_fusion.12), channel_id=1, source_target_pairs={{0,2},{1,3},{2,0},{3,1},{4,6},{5,7},{6,4},{7,5},{8,10},{9,11},{10,... | collective-permute-start | bytes 98312 | tf_op jit(solution)/shard_map/ppermute | solution.py:95
  41.1 9.5 %collective-permute-start.5 = (f32[16,512]{1,0:T(8,128)S(1)}, f32[16,512]{1,0:T(8,128)S(1)}, u32[]{:S(2)}, u32[]{:S(2)}) collective-permute-start(f32[16,512]{1,0:T(8,128)S(1)} %fusion.1), channel_id=1, source_target_pairs={{0,2},{1,3},{2,0},{3,1},{4,6},{5,7},{6,4},{7,5},{8,10},{9,11},{10,... | collective-permute-start | bytes 98312 | tf_op jit(solution)/shard_map/ppermute | solution.py:95
  50.8 11.0 %collective-permute-start.24 = (f32[128,384]{1,0:T(8,128)S(1)}, f32[128,384]{1,0:T(8,128)S(1)}, u32[]{:S(2)}, u32[]{:S(2)}) collective-permute-start(f32[128,384]{1,0:T(8,128)S(1)} %pad_maximum_fusion.3), channel_id=1, source_target_pairs={{0,8},{1,9},{2,10},{3,11},{4,20},{5,21},{6,22},{7,23},{8,0},{9,1},... | collective-permute-start | bytes 589832 | tf_op jit(solution)/shard_map/ppermute | solution.py:95
  52.9 6.4 %collective-permute-start.15 = (f32[64,512]{1,0:T(8,128)S(1)}, f32[64,512]{1,0:T(8,128)S(1)}, u32[]{:S(2)}, u32[]{:S(2)}) collective-permute-start(f32[64,512]{1,0:T(8,128)S(1)} %pad_maximum_fusion.5), channel_id=1, source_target_pairs={{0,16},{1,17},{2,18},{3,19},{4,12},{5,13},{6,14},{7,15},{8,24},{9,... | collective-permute-start | bytes 393224 | tf_op jit(solution)/shard_map/ppermute | solution.py:95
  55.0 6.1 %collective-permute-start.7 = (f32[64,512]{1,0:T(8,128)S(1)}, f32[64,512]{1,0:T(8,128)S(1)}, u32[]{:S(2)}, u32[]{:S(2)}) collective-permute-start(f32[64,512]{1,0:T(8,128)S(1)} %pad_maximum_fusion.4), channel_id=1, source_target_pairs={{0,16},{1,17},{2,18},{3,19},{4,12},{5,13},{6,14},{7,15},{8,24},{9,... | collective-permute-start | bytes 393224 | tf_op jit(solution)/shard_map/ppermute | solution.py:95
  59.3 9.3 %collective-permute-start.16 = (f32[128,512]{1,0:T(8,128)S(1)}, f32[128,512]{1,0:T(8,128)S(1)}, u32[]{:S(2)}, u32[]{:S(2)}) collective-permute-start(f32[128,512]{1,0:T(8,128)S(1)} %pad_maximum_fusion.2), channel_id=1, source_target_pairs={{0,8},{1,9},{2,10},{3,11},{4,20},{5,21},{6,22},{7,23},{8,0},{9,1},... | collective-permute-start | bytes 786440 | tf_op jit(solution)/shard_map/ppermute | solution.py:95
  61.1 7.5 %collective-permute-start.8 = (f32[128,512]{1,0:T(8,128)S(1)}, f32[128,512]{1,0:T(8,128)S(1)}, u32[]{:S(2)}, u32[]{:S(2)}) collective-permute-start(f32[128,512]{1,0:T(8,128)S(1)} %pad_maximum_fusion.1), channel_id=1, source_target_pairs={{0,8},{1,9},{2,10},{3,11},{4,20},{5,21},{6,22},{7,23},{8,0},{9,1},... | collective-permute-start | bytes 786440 | tf_op jit(solution)/shard_map/ppermute | solution.py:95
  72.2 5.0 %collective-permute-start.27 = (f32[160,128]{1,0:T(8,128)S(1)}, f32[160,128]{1,0:T(8,128)S(1)}, u32[]{:S(2)}, u32[]{:S(2)}) collective-permute-start(f32[160,128]{1,0:T(8,128)S(1)} %get-tuple-element.25), channel_id=1, source_target_pairs={{0,16},{1,17},{2,18},{3,19},{4,12},{5,13},{6,14},{7,15},{8,24},{9,... | collective-permute-start | bytes 245768 | tf_op jit(solution)/shard_map/ppermute | solution.py:95
  73.0 5.2 %collective-permute-start.28 = (f32[160,128]{1,0:T(8,128)S(1)}, f32[160,128]{1,0:T(8,128)S(1)}, u32[]{:S(2)}, u32[]{:S(2)}) collective-permute-start(f32[160,128]{1,0:T(8,128)S(1)} %get-tuple-element.26), channel_id=1, source_target_pairs={{0,8},{1,9},{2,10},{3,11},{4,20},{5,21},{6,22},{7,23},{8,0},{9,1},... | collective-permute-start | bytes 245768 | tf_op jit(solution)/shard_map/ppermute | solution.py:95
  74.3 5.7 %collective-permute-start.29 = (f32[160,128]{1,0:T(8,128)S(1)}, f32[160,128]{1,0:T(8,128)S(1)}, u32[]{:S(2)}, u32[]{:S(2)}) collective-permute-start(f32[160,128]{1,0:T(8,128)S(1)} %get-tuple-element.27), channel_id=1, source_target_pairs={{0,24},{1,25},{2,26},{3,27},{4,28},{5,29},{6,30},{7,31},{8,16},{9,... | collective-permute-start | bytes 245768 | tf_op jit(solution)/shard_map/ppermute | solution.py:95
  80.0 7.3 %collective-permute-start.32 = (f32[160,128]{1,0:T(8,128)S(1)}, f32[160,128]{1,0:T(8,128)S(1)}, u32[]{:S(2)}, u32[]{:S(2)}) collective-permute-start(f32[160,128]{1,0:T(8,128)S(1)} %add_add_fusion.1), channel_id=1, source_target_pairs={{0,3},{1,2},{2,1},{3,0},{4,7},{5,6},{6,5},{7,4},{8,11},{9,10},{10,... | collective-permute-start | bytes 245768 | tf_op jit(solution)/shard_map/ppermute | solution.py:95
  81.6 5.6 %collective-permute-start.31 = (f32[160,128]{1,0:T(8,128)S(1)}, f32[160,128]{1,0:T(8,128)S(1)}, u32[]{:S(2)}, u32[]{:S(2)}) collective-permute-start(f32[160,128]{1,0:T(8,128)S(1)} %add_add_fusion.1), channel_id=1, source_target_pairs={{0,1},{1,0},{2,3},{3,2},{4,5},{5,4},{6,7},{7,6},{8,9},{9,8},{10,11... | collective-permute-start | bytes 245768 | tf_op jit(solution)/shard_map/ppermute | solution.py:95
  81.6 8.2 %collective-permute-start.30 = (f32[160,128]{1,0:T(8,128)S(1)}, f32[160,128]{1,0:T(8,128)S(1)}, u32[]{:S(2)}, u32[]{:S(2)}) collective-permute-start(f32[160,128]{1,0:T(8,128)S(1)} %add_add_fusion.1), channel_id=1, source_target_pairs={{0,2},{1,3},{2,0},{3,1},{4,6},{5,7},{6,4},{7,5},{8,10},{9,11},{10,... | collective-permute-start | bytes 245768 | tf_op jit(solution)/shard_map/ppermute | solution.py:95
  89.8 5.4 %collective-permute-start.35 = (f32[160,128]{1,0:T(8,128)S(1)}, f32[160,128]{1,0:T(8,128)S(1)}, u32[]{:S(2)}, u32[]{:S(2)}) collective-permute-start(f32[160,128]{1,0:T(8,128)S(1)} %add_add_fusion), channel_id=1, source_target_pairs={{0,24},{1,25},{2,26},{3,27},{4,28},{5,29},{6,30},{7,31},{8,16},{9,... | collective-permute-start | bytes 245768 | tf_op jit(solution)/shard_map/ppermute | solution.py:95
  (14 other events, 49.2 us)
where the time goes:
time: 111 us
  starting transfers between devices  46.5 us (42%)
  waiting for transfers between devices  43.9 us (40%)
  Pallas kernels  18.3 us (16%)
  local copies, waits for them, and re-layouts  1.25 us (1%)
    ppermute x37, starting transfers between devices, swap(): return lax.ppermute(x, AXES, perm)  46.5 us
    ppermute x37, waiting for transfers between devices, swap(): return lax.ppermute(x, AXES, perm)  43.9 us
    pallas_call x9, Pallas kernels, call(): pl.pallas_call(kernel, cost_estimate=pl.CostEstimate(flops=flops, bytes_a...  18.3 us
  transfers between devices with their start and end apart: 37, of which 25 were waited for; matrix products, arithmetic and copies ran while one was open for 0% of the time, Pallas kernels for 3%

commit v1 on v0

--- a/solution.py
+++ b/solution.py
@@ -138,8 +138,9 @@
 def project_kernel(j, left_ref, own_ref, peer_ref, keep_ref, send_ref):
     half = keep_ref.shape[0]
     right = stacked(jnp.concatenate([own_ref[j], peer_ref[j]], axis=1), axis=1)[1]
-    keep_ref[...] = bf16_dot(left_ref[:half, :], right, NT)
-    send_ref[...] = bf16_dot(left_ref[half:, :], right, NT)
+    both = bf16_dot(left_ref[...], right, NT)
+    keep_ref[...] = both[:half, :]
+    send_ref[...] = both[half:, :]
 
 
 def first_project_kernel(route, scatter, own_ref, peer_ref, keep_ref, send_ref, left_ref, left, right):

time: 111 us -> 110 us (level)
  starting transfers between devices: 46.5 us -> 48.7 us
  waiting for transfers between devices: 43.9 us -> 42.1 us
    ppermute x37, starting transfers between devices: 46.5 us -> 48.7 us  [swap(): return lax.ppermute(x, AXES, perm)]
    ppermute x37, waiting for transfers between devices: 43.9 us -> 42.1 us  [swap(): return lax.ppermute(x, AXES, perm)]
  transfers between devices with their start and end apart: 37 -> 37, of which waited for: 25 -> 26; matrix products, arithmetic and copies ran while one was open for 0% -> 0% of each run, Pallas kernels for 3% -> 2%
where the time goes in v1:
time: 110 us
  starting transfers between devices  48.7 us (44%)
  waiting for transfers between devices  42.1 us (38%)
  Pallas kernels  17.2 us (16%)
  local copies, waits for them, and re-layouts  1.25 us (1%)
    ppermute x37, starting transfers between devices, swap(): return lax.ppermute(x, AXES, perm)  48.7 us
    ppermute x37, waiting for transfers between devices, swap(): return lax.ppermute(x, AXES, perm)  42.1 us
    pallas_call x9, Pallas kernels, call(): pl.pallas_call(kernel, cost_estimate=pl.CostEstimate(flops=flops, bytes_a...  17.2 us
  transfers between devices with their start and end apart: 37, of which 26 were waited for; matrix products, arithmetic and copies ran while one was open for 0% of the time, Pallas kernels for 2%

profile of v1, /device:TPU:0, one launch (start us, length us, event | category | flops | bytes accessed | tf_op | source)
XLA Modules:
  0.0 110.0 jit_solution(5484727696534970201)
XLA Ops:
  3.6 2.9 %collective-permute-start.17 = (f32[128,384]{1,0:T(8,128)S(1)}, f32[128,384]{1,0:T(8,128)S(1)}, u32[]{:S(2)}, u32[]{:S(2)}) collective-permute-start(f32[128,384]{1,0:T(8,128)S(1)} %get-tuple-element.23), channel_id=1, source_target_pairs={{0,8},{1,9},{2,10},{3,11},{4,20},{5,21},{6,22},{7,23},{8,0},{9,1},... | collective-permute-start | bytes 589832 | tf_op jit(solution)/shard_map/ppermute | solution.py:95
  6.5 3.6 %collective-permute-done.17 = f32[128,384]{1,0:T(8,128)S(1)} collective-permute-done((f32[128,384]{1,0:T(8,128)S(1)}, f32[128,384]{1,0:T(8,128)S(1)}, u32[]{:S(2)}, u32[]{:S(2)}) %collective-permute-start.17) | collective-permute-done | bytes 196640 | tf_op jit(solution)/shard_map/ppermute | solution.py:95
  10.2 2.1 %collective-permute-start.18 = (f32[64,384]{1,0:T(8,128)S(1)}, f32[64,384]{1,0:T(8,128)S(1)}, u32[]{:S(2)}, u32[]{:S(2)}) collective-permute-start(f32[64,384]{1,0:T(8,128)S(1)} %get-tuple-element.34), channel_id=1, source_target_pairs={{0,16},{1,17},{2,18},{3,19},{4,12},{5,13},{6,14},{7,15},{8,24},{9,... | collective-permute-start | bytes 294920 | tf_op jit(solution)/shard_map/ppermute | solution.py:95
  15.7 2.2 %collective-permute-start.19 = (f32[32,384]{1,0:T(8,128)S(1)}, f32[32,384]{1,0:T(8,128)S(1)}, u32[]{:S(2)}, u32[]{:S(2)}) collective-permute-start(f32[32,384]{1,0:T(8,128)S(1)} %get-tuple-element.40), channel_id=1, source_target_pairs={{0,1},{1,0},{2,3},{3,2},{4,5},{5,4},{6,7},{7,6},{8,9},{9,8},{10,11... | collective-permute-start | bytes 147464 | tf_op jit(solution)/shard_map/ppermute | solution.py:95
  20.0 3.0 %collective-permute-start.20 = (f32[16,384]{1,0:T(8,128)S(1)}, f32[16,384]{1,0:T(8,128)S(1)}, u32[]{:S(2)}, u32[]{:S(2)}) collective-permute-start(f32[16,384]{1,0:T(8,128)S(1)} %slice_add_fusion.16), channel_id=1, source_target_pairs={{0,2},{1,3},{2,0},{3,1},{4,6},{5,7},{6,4},{7,5},{8,10},{9,11},{10,... | collective-permute-start | bytes 73736 | tf_op jit(solution)/shard_map/ppermute | solution.py:95
  24.8 2.9 %collective-permute-start.21 = (f32[16,384]{1,0:T(8,128)S(1)}, f32[16,384]{1,0:T(8,128)S(1)}, u32[]{:S(2)}, u32[]{:S(2)}) collective-permute-start(f32[16,384]{1,0:T(8,128)S(1)} %fusion.2), channel_id=1, source_target_pairs={{0,2},{1,3},{2,0},{3,1},{4,6},{5,7},{6,4},{7,5},{8,10},{9,11},{10,... | collective-permute-start | bytes 73736 | tf_op jit(solution)/shard_map/ppermute | solution.py:95
  27.8 1.8 %collective-permute-start.11 = (f32[32,512]{1,0:T(8,128)S(1)}, f32[32,512]{1,0:T(8,128)S(1)}, u32[]{:S(2)}, u32[]{:S(2)}) collective-permute-start(f32[32,512]{1,0:T(8,128)S(1)} %get-tuple-element.36), channel_id=1, source_target_pairs={{0,1},{1,0},{2,3},{3,2},{4,5},{5,4},{6,7},{7,6},{8,9},{9,8},{10,11... | collective-permute-start | bytes 196616 | tf_op jit(solution)/shard_map/ppermute | solution.py:95
  30.0 1.7 %collective-permute-start.22 = (f32[32,384]{1,0:T(8,128)S(1)}, f32[32,384]{1,0:T(8,128)S(1)}, u32[]{:S(2)}, u32[]{:S(2)}) collective-permute-start(f32[32,384]{1,0:T(8,128)S(1)} %pad_maximum_fusion.9), channel_id=1, source_target_pairs={{0,1},{1,0},{2,3},{3,2},{4,5},{5,4},{6,7},{7,6},{8,9},{9,8},{10,11... | collective-permute-start | bytes 147464 | tf_op jit(solution)/shard_map/ppermute | solution.py:95
  31.7 2.7 %collective-permute-done.22 = f32[32,384]{1,0:T(8,128)S(1)} collective-permute-done((f32[32,384]{1,0:T(8,128)S(1)}, f32[32,384]{1,0:T(8,128)S(1)}, u32[]{:S(2)}, u32[]{:S(2)}) %collective-permute-start.22) | collective-permute-done | bytes 49184 | tf_op jit(solution)/shard_map/ppermute | solution.py:95
  36.1 2.4 %collective-permute-start.4 = (f32[16,512]{1,0:T(8,128)S(1)}, f32[16,512]{1,0:T(8,128)S(1)}, u32[]{:S(2)}, u32[]{:S(2)}) collective-permute-start(f32[16,512]{1,0:T(8,128)S(1)} %slice_add_fusion.14), channel_id=1, source_target_pairs={{0,2},{1,3},{2,0},{3,1},{4,6},{5,7},{6,4},{7,5},{8,10},{9,11},{10,... | collective-permute-start | bytes 98312 | tf_op jit(solution)/shard_map/ppermute | solution.py:95
  39.1 1.8 %collective-permute-done.4 = f32[16,512]{1,0:T(8,128)S(1)} collective-permute-done((f32[16,512]{1,0:T(8,128)S(1)}, f32[16,512]{1,0:T(8,128)S(1)}, u32[]{:S(2)}, u32[]{:S(2)}) %collective-permute-start.4) | collective-permute-done | bytes 32800 | tf_op jit(solution)/shard_map/ppermute | solution.py:95
  41.0 2.4 %collective-permute-start.5 = (f32[16,512]{1,0:T(8,128)S(1)}, f32[16,512]{1,0:T(8,128)S(1)}, u32[]{:S(2)}, u32[]{:S(2)}) collective-permute-start(f32[16,512]{1,0:T(8,128)S(1)} %fusion.1), channel_id=1, source_target_pairs={{0,2},{1,3},{2,0},{3,1},{4,6},{5,7},{6,4},{7,5},{8,10},{9,11},{10,... | collective-permute-start | bytes 98312 | tf_op jit(solution)/shard_map/ppermute | solution.py:95
  44.1 4.1 %collective-permute-done.13 = f32[16,512]{1,0:T(8,128)S(1)} collective-permute-done((f32[16,512]{1,0:T(8,128)S(1)}, f32[16,512]{1,0:T(8,128)S(1)}, u32[]{:S(2)}, u32[]{:S(2)}) %collective-permute-start.13) | collective-permute-done | bytes 32800 | tf_op jit(solution)/shard_map/ppermute | solution.py:95
  48.3 2.4 %collective-permute-start.14 = (f32[32,512]{1,0:T(8,128)S(1)}, f32[32,512]{1,0:T(8,128)S(1)}, u32[]{:S(2)}, u32[]{:S(2)}) collective-permute-start(f32[32,512]{1,0:T(8,128)S(1)} %pad_maximum_fusion.8), channel_id=1, source_target_pairs={{0,1},{1,0},{2,3},{3,2},{4,5},{5,4},{6,7},{7,6},{8,9},{9,8},{10,11... | collective-permute-start | bytes 196616 | tf_op jit(solution)/shard_map/ppermute | solution.py:95
  55.9 2.4 %collective-permute-done.15 = f32[64,512]{1,0:T(8,128)S(1)} collective-permute-done((f32[64,512]{1,0:T(8,128)S(1)}, f32[64,512]{1,0:T(8,128)S(1)}, u32[]{:S(2)}, u32[]{:S(2)}) %collective-permute-start.15) | collective-permute-done | bytes 131104 | tf_op jit(solution)/shard_map/ppermute | solution.py:95
  63.6 4.0 %collective-permute-done.8 = f32[128,512]{1,0:T(8,128)S(1)} collective-permute-done((f32[128,512]{1,0:T(8,128)S(1)}, f32[128,512]{1,0:T(8,128)S(1)}, u32[]{:S(2)}, u32[]{:S(2)}) %collective-permute-start.8) | collective-permute-done | bytes 262176 | tf_op jit(solution)/shard_map/ppermute | solution.py:95
  71.2 1.8 %collective-permute-start.27 = (f32[160,128]{1,0:T(8,128)S(1)}, f32[160,128]{1,0:T(8,128)S(1)}, u32[]{:S(2)}, u32[]{:S(2)}) collective-permute-start(f32[160,128]{1,0:T(8,128)S(1)} %get-tuple-element.25), channel_id=1, source_target_pairs={{0,16},{1,17},{2,18},{3,19},{4,12},{5,13},{6,14},{7,15},{8,24},{9,... | collective-permute-start | bytes 245768 | tf_op jit(solution)/shard_map/ppermute | solution.py:95
  74.8 1.7 %collective-permute-done.27 = f32[160,128]{1,0:T(8,128)S(1)} collective-permute-done((f32[160,128]{1,0:T(8,128)S(1)}, f32[160,128]{1,0:T(8,128)S(1)}, u32[]{:S(2)}, u32[]{:S(2)}) %collective-permute-start.27) | collective-permute-done | bytes 81952 | tf_op jit(solution)/shard_map/ppermute | solution.py:95
  81.0 3.0 %collective-permute-start.30 = (f32[160,128]{1,0:T(8,128)S(1)}, f32[160,128]{1,0:T(8,128)S(1)}, u32[]{:S(2)}, u32[]{:S(2)}) collective-permute-start(f32[160,128]{1,0:T(8,128)S(1)} %add_add_fusion.1), channel_id=1, source_target_pairs={{0,2},{1,3},{2,0},{3,1},{4,6},{5,7},{6,4},{7,5},{8,10},{9,11},{10,... | collective-permute-start | bytes 245768 | tf_op jit(solution)/shard_map/ppermute | solution.py:95
  84.0 2.1 %collective-permute-done.32 = f32[160,128]{1,0:T(8,128)S(1)} collective-permute-done((f32[160,128]{1,0:T(8,128)S(1)}, f32[160,128]{1,0:T(8,128)S(1)}, u32[]{:S(2)}, u32[]{:S(2)}) %collective-permute-start.32) | collective-permute-done | bytes 81952 | tf_op jit(solution)/shard_map/ppermute | solution.py:95
  86.6 2.2 %collective-permute-done.30 = f32[160,128]{1,0:T(8,128)S(1)} collective-permute-done((f32[160,128]{1,0:T(8,128)S(1)}, f32[160,128]{1,0:T(8,128)S(1)}, u32[]{:S(2)}, u32[]{:S(2)}) %collective-permute-start.30) | collective-permute-done | bytes 81952 | tf_op jit(solution)/shard_map/ppermute | solution.py:95
  92.3 1.9 %collective-permute-done.35 = f32[160,128]{1,0:T(8,128)S(1)} collective-permute-done((f32[160,128]{1,0:T(8,128)S(1)}, f32[160,128]{1,0:T(8,128)S(1)}, u32[]{:S(2)}, u32[]{:S(2)}) %collective-permute-start.35) | collective-permute-done | bytes 81952 | tf_op jit(solution)/shard_map/ppermute | solution.py:95
  96.1 1.6 %collective-permute-done.36.other_ref = f32[640,128]{1,0:T(8,128)S(1)} collective-permute-done((f32[640,128]{1,0:T(8,128)S(1)}, f32[640,128]{1,0:T(8,128)S(1)}, u32[]{:S(2)}, u32[]{:S(2)}) %collective-permute-start.36) | collective-permute-done | bytes 327712 | tf_op jit(solution)/shard_map/ppermute | solution.py:95
  97.7 12.3 %shard_map.25 = f32[512,128]{1,0:T(8,128)} custom-call(f32[640,128]{1,0:T(8,128)S(1)} %pad_maximum_fusion.mine_ref, f32[640,128]{1,0:T(8,128)S(1)} %collective-permute-done.36.other_ref, f32[512,128]{1,0:T(8,128)S(1)} %get-tuple-element.28.p_ref), custom_call_target="tpu_custom_call" | custom-call | bytes 1179648 | tf_op jit(solution)/shard_map/pallas_call | solution.py:338
  (101 shorter events, 40.5 us)
Async XLA Ops:
  3.6 6.6 %collective-permute-start.17 = (f32[128,384]{1,0:T(8,128)S(1)}, f32[128,384]{1,0:T(8,128)S(1)}, u32[]{:S(2)}, u32[]{:S(2)}) collective-permute-start(f32[128,384]{1,0:T(8,128)S(1)} %get-tuple-element.23), channel_id=1, source_target_pairs={{0,8},{1,9},{2,10},{3,11},{4,20},{5,21},{6,22},{7,23},{8,0},{9,1},... | collective-permute-start | bytes 589832 | tf_op jit(solution)/shard_map/ppermute | solution.py:95
  10.2 5.5 %collective-permute-start.18 = (f32[64,384]{1,0:T(8,128)S(1)}, f32[64,384]{1,0:T(8,128)S(1)}, u32[]{:S(2)}, u32[]{:S(2)}) collective-permute-start(f32[64,384]{1,0:T(8,128)S(1)} %get-tuple-element.34), channel_id=1, source_target_pairs={{0,16},{1,17},{2,18},{3,19},{4,12},{5,13},{6,14},{7,15},{8,24},{9,... | collective-permute-start | bytes 294920 | tf_op jit(solution)/shard_map/ppermute | solution.py:95
  12.9 6.4 %collective-permute-start.9 = (f32[128,512]{1,0:T(8,128)S(1)}, f32[128,512]{1,0:T(8,128)S(1)}, u32[]{:S(2)}, u32[]{:S(2)}) collective-permute-start(f32[128,512]{1,0:T(8,128)S(1)} %get-tuple-element.21), channel_id=1, source_target_pairs={{0,8},{1,9},{2,10},{3,11},{4,20},{5,21},{6,22},{7,23},{8,0},{9,1},... | collective-permute-start | bytes 786440 | tf_op jit(solution)/shard_map/ppermute | solution.py:95
  15.1 8.5 %collective-permute-start.1 = (f32[128,512]{1,0:T(8,128)S(1)}, f32[128,512]{1,0:T(8,128)S(1)}, u32[]{:S(2)}, u32[]{:S(2)}) collective-permute-start(f32[128,512]{1,0:T(8,128)S(1)} %get-tuple-element.19), channel_id=1, source_target_pairs={{0,8},{1,9},{2,10},{3,11},{4,20},{5,21},{6,22},{7,23},{8,0},{9,1},... | collective-permute-start | bytes 786440 | tf_op jit(solution)/shard_map/ppermute | solution.py:95
  19.4 8.4 %collective-permute-start.10 = (f32[64,512]{1,0:T(8,128)S(1)}, f32[64,512]{1,0:T(8,128)S(1)}, u32[]{:S(2)}, u32[]{:S(2)}) collective-permute-start(f32[64,512]{1,0:T(8,128)S(1)} %get-tuple-element.30), channel_id=1, source_target_pairs={{0,16},{1,17},{2,18},{3,19},{4,12},{5,13},{6,14},{7,15},{8,24},{9,... | collective-permute-start | bytes 393224 | tf_op jit(solution)/shard_map/ppermute | solution.py:95
  23.6 6.0 %collective-permute-start.2 = (f32[64,512]{1,0:T(8,128)S(1)}, f32[64,512]{1,0:T(8,128)S(1)}, u32[]{:S(2)}, u32[]{:S(2)}) collective-permute-start(f32[64,512]{1,0:T(8,128)S(1)} %get-tuple-element.32), channel_id=1, source_target_pairs={{0,16},{1,17},{2,18},{3,19},{4,12},{5,13},{6,14},{7,15},{8,24},{9,... | collective-permute-start | bytes 393224 | tf_op jit(solution)/shard_map/ppermute | solution.py:95
  24.8 5.2 %collective-permute-start.21 = (f32[16,384]{1,0:T(8,128)S(1)}, f32[16,384]{1,0:T(8,128)S(1)}, u32[]{:S(2)}, u32[]{:S(2)}) collective-permute-start(f32[16,384]{1,0:T(8,128)S(1)} %fusion.2), channel_id=1, source_target_pairs={{0,2},{1,3},{2,0},{3,1},{4,6},{5,7},{6,4},{7,5},{8,10},{9,11},{10,... | collective-permute-start | bytes 73736 | tf_op jit(solution)/shard_map/ppermute | solution.py:95
  27.8 10.7 %collective-permute-start.11 = (f32[32,512]{1,0:T(8,128)S(1)}, f32[32,512]{1,0:T(8,128)S(1)}, u32[]{:S(2)}, u32[]{:S(2)}) collective-permute-start(f32[32,512]{1,0:T(8,128)S(1)} %get-tuple-element.36), channel_id=1, source_target_pairs={{0,1},{1,0},{2,3},{3,2},{4,5},{5,4},{6,7},{7,6},{8,9},{9,8},{10,11... | collective-permute-start | bytes 196616 | tf_op jit(solution)/shard_map/ppermute | solution.py:95
  29.6 6.5 %collective-permute-start.3 = (f32[32,512]{1,0:T(8,128)S(1)}, f32[32,512]{1,0:T(8,128)S(1)}, u32[]{:S(2)}, u32[]{:S(2)}) collective-permute-start(f32[32,512]{1,0:T(8,128)S(1)} %get-tuple-element.38), channel_id=1, source_target_pairs={{0,1},{1,0},{2,3},{3,2},{4,5},{5,4},{6,7},{7,6},{8,9},{9,8},{10,11... | collective-permute-start | bytes 196616 | tf_op jit(solution)/shard_map/ppermute | solution.py:95
  34.4 16.4 %collective-permute-start.23 = (f32[64,384]{1,0:T(8,128)S(1)}, f32[64,384]{1,0:T(8,128)S(1)}, u32[]{:S(2)}, u32[]{:S(2)}) collective-permute-start(f32[64,384]{1,0:T(8,128)S(1)} %pad_maximum_fusion.6), channel_id=1, source_target_pairs={{0,16},{1,17},{2,18},{3,19},{4,12},{5,13},{6,14},{7,15},{8,24},{9,... | collective-permute-start | bytes 294920 | tf_op jit(solution)/shard_map/ppermute | solution.py:95
  36.1 4.9 %collective-permute-start.4 = (f32[16,512]{1,0:T(8,128)S(1)}, f32[16,512]{1,0:T(8,128)S(1)}, u32[]{:S(2)}, u32[]{:S(2)}) collective-permute-start(f32[16,512]{1,0:T(8,128)S(1)} %slice_add_fusion.14), channel_id=1, source_target_pairs={{0,2},{1,3},{2,0},{3,1},{4,6},{5,7},{6,4},{7,5},{8,10},{9,11},{10,... | collective-permute-start | bytes 98312 | tf_op jit(solution)/shard_map/ppermute | solution.py:95
  38.5 4.9 %collective-permute-start.12 = (f32[16,512]{1,0:T(8,128)S(1)}, f32[16,512]{1,0:T(8,128)S(1)}, u32[]{:S(2)}, u32[]{:S(2)}) collective-permute-start(f32[16,512]{1,0:T(8,128)S(1)} %slice_add_fusion.12), channel_id=1, source_target_pairs={{0,2},{1,3},{2,0},{3,1},{4,6},{5,7},{6,4},{7,5},{8,10},{9,11},{10,... | collective-permute-start | bytes 98312 | tf_op jit(solution)/shard_map/ppermute | solution.py:95
  41.0 9.8 %collective-permute-start.5 = (f32[16,512]{1,0:T(8,128)S(1)}, f32[16,512]{1,0:T(8,128)S(1)}, u32[]{:S(2)}, u32[]{:S(2)}) collective-permute-start(f32[16,512]{1,0:T(8,128)S(1)} %fusion.1), channel_id=1, source_target_pairs={{0,2},{1,3},{2,0},{3,1},{4,6},{5,7},{6,4},{7,5},{8,10},{9,11},{10,... | collective-permute-start | bytes 98312 | tf_op jit(solution)/shard_map/ppermute | solution.py:95
  50.8 10.6 %collective-permute-start.24 = (f32[128,384]{1,0:T(8,128)S(1)}, f32[128,384]{1,0:T(8,128)S(1)}, u32[]{:S(2)}, u32[]{:S(2)}) collective-permute-start(f32[128,384]{1,0:T(8,128)S(1)} %pad_maximum_fusion.3), channel_id=1, source_target_pairs={{0,8},{1,9},{2,10},{3,11},{4,20},{5,21},{6,22},{7,23},{8,0},{9,1},... | collective-permute-start | bytes 589832 | tf_op jit(solution)/shard_map/ppermute | solution.py:95
  53.0 5.4 %collective-permute-start.15 = (f32[64,512]{1,0:T(8,128)S(1)}, f32[64,512]{1,0:T(8,128)S(1)}, u32[]{:S(2)}, u32[]{:S(2)}) collective-permute-start(f32[64,512]{1,0:T(8,128)S(1)} %pad_maximum_fusion.5), channel_id=1, source_target_pairs={{0,16},{1,17},{2,18},{3,19},{4,12},{5,13},{6,14},{7,15},{8,24},{9,... | collective-permute-start | bytes 393224 | tf_op jit(solution)/shard_map/ppermute | solution.py:95
  55.1 5.0 %collective-permute-start.7 = (f32[64,512]{1,0:T(8,128)S(1)}, f32[64,512]{1,0:T(8,128)S(1)}, u32[]{:S(2)}, u32[]{:S(2)}) collective-permute-start(f32[64,512]{1,0:T(8,128)S(1)} %pad_maximum_fusion.4), channel_id=1, source_target_pairs={{0,16},{1,17},{2,18},{3,19},{4,12},{5,13},{6,14},{7,15},{8,24},{9,... | collective-permute-start | bytes 393224 | tf_op jit(solution)/shard_map/ppermute | solution.py:95
  58.4 9.3 %collective-permute-start.16 = (f32[128,512]{1,0:T(8,128)S(1)}, f32[128,512]{1,0:T(8,128)S(1)}, u32[]{:S(2)}, u32[]{:S(2)}) collective-permute-start(f32[128,512]{1,0:T(8,128)S(1)} %pad_maximum_fusion.2), channel_id=1, source_target_pairs={{0,8},{1,9},{2,10},{3,11},{4,20},{5,21},{6,22},{7,23},{8,0},{9,1},... | collective-permute-start | bytes 786440 | tf_op jit(solution)/shard_map/ppermute | solution.py:95
  60.1 7.5 %collective-permute-start.8 = (f32[128,512]{1,0:T(8,128)S(1)}, f32[128,512]{1,0:T(8,128)S(1)}, u32[]{:S(2)}, u32[]{:S(2)}) collective-permute-start(f32[128,512]{1,0:T(8,128)S(1)} %pad_maximum_fusion.1), channel_id=1, source_target_pairs={{0,8},{1,9},{2,10},{3,11},{4,20},{5,21},{6,22},{7,23},{8,0},{9,1},... | collective-permute-start | bytes 786440 | tf_op jit(solution)/shard_map/ppermute | solution.py:95
  71.2 5.3 %collective-permute-start.27 = (f32[160,128]{1,0:T(8,128)S(1)}, f32[160,128]{1,0:T(8,128)S(1)}, u32[]{:S(2)}, u32[]{:S(2)}) collective-permute-start(f32[160,128]{1,0:T(8,128)S(1)} %get-tuple-element.25), channel_id=1, source_target_pairs={{0,16},{1,17},{2,18},{3,19},{4,12},{5,13},{6,14},{7,15},{8,24},{9,... | collective-permute-start | bytes 245768 | tf_op jit(solution)/shard_map/ppermute | solution.py:95
  74.2 5.3 %collective-permute-start.29 = (f32[160,128]{1,0:T(8,128)S(1)}, f32[160,128]{1,0:T(8,128)S(1)}, u32[]{:S(2)}, u32[]{:S(2)}) collective-permute-start(f32[160,128]{1,0:T(8,128)S(1)} %get-tuple-element.27), channel_id=1, source_target_pairs={{0,24},{1,25},{2,26},{3,27},{4,28},{5,29},{6,30},{7,31},{8,16},{9,... | collective-permute-start | bytes 245768 | tf_op jit(solution)/shard_map/ppermute | solution.py:95
  79.6 6.6 %collective-permute-start.32 = (f32[160,128]{1,0:T(8,128)S(1)}, f32[160,128]{1,0:T(8,128)S(1)}, u32[]{:S(2)}, u32[]{:S(2)}) collective-permute-start(f32[160,128]{1,0:T(8,128)S(1)} %add_add_fusion.1), channel_id=1, source_target_pairs={{0,3},{1,2},{2,1},{3,0},{4,7},{5,6},{6,5},{7,4},{8,11},{9,10},{10,... | collective-permute-start | bytes 245768 | tf_op jit(solution)/shard_map/ppermute | solution.py:95
  81.0 5.6 %collective-permute-start.31 = (f32[160,128]{1,0:T(8,128)S(1)}, f32[160,128]{1,0:T(8,128)S(1)}, u32[]{:S(2)}, u32[]{:S(2)}) collective-permute-start(f32[160,128]{1,0:T(8,128)S(1)} %add_add_fusion.1), channel_id=1, source_target_pairs={{0,1},{1,0},{2,3},{3,2},{4,5},{5,4},{6,7},{7,6},{8,9},{9,8},{10,11... | collective-permute-start | bytes 245768 | tf_op jit(solution)/shard_map/ppermute | solution.py:95
  81.0 7.7 %collective-permute-start.30 = (f32[160,128]{1,0:T(8,128)S(1)}, f32[160,128]{1,0:T(8,128)S(1)}, u32[]{:S(2)}, u32[]{:S(2)}) collective-permute-start(f32[160,128]{1,0:T(8,128)S(1)} %add_add_fusion.1), channel_id=1, source_target_pairs={{0,2},{1,3},{2,0},{3,1},{4,6},{5,7},{6,4},{7,5},{8,10},{9,11},{10,... | collective-permute-start | bytes 245768 | tf_op jit(solution)/shard_map/ppermute | solution.py:95
  88.8 5.4 %collective-permute-start.35 = (f32[160,128]{1,0:T(8,128)S(1)}, f32[160,128]{1,0:T(8,128)S(1)}, u32[]{:S(2)}, u32[]{:S(2)}) collective-permute-start(f32[160,128]{1,0:T(8,128)S(1)} %add_add_fusion), channel_id=1, source_target_pairs={{0,24},{1,25},{2,26},{3,27},{4,28},{5,29},{6,30},{7,31},{8,16},{9,... | collective-permute-start | bytes 245768 | tf_op jit(solution)/shard_map/ppermute | solution.py:95
  (14 other events, 49.7 us)

commit v2 on v0

--- a/solution.py
+++ b/solution.py
@@ -8,7 +8,6 @@
 from jax.sharding import PartitionSpec as P
 
 
-HIGHEST = lax.Precision.HIGHEST
 WEIGHTS = (2.5, -2.0, 0.5)
 TILE = 128
 PANEL = 32
@@ -19,10 +18,6 @@
 NT = (((1,), (1,)), ((), ()))
 NN = (((1,), (0,)), ((), ()))
 TN = (((0,), (0,)), ((), ()))
-
-
-def dot(a, b, dims):
-    return lax.dot_general(a, b, dims, precision=HIGHEST, preferred_element_type=jnp.float32)
 
 
 def bf16_dot(a, b, dims):
@@ -221,7 +216,7 @@
 
 
 def gram_kernel(route, scale, mine_ref, other_ref, *refs):
-    outs, own_ref, p, acc = refs[:-3], refs[-3], refs[-2], refs[-1]
+    outs, own_ref, p, acc, left, right = refs[:-5], *refs[-5:]
     half, width = mine_ref.shape[0], own_ref.shape[1]
     count = 2 * half // TILE
     lists = core_blocks(count)
@@ -233,14 +228,15 @@
     p[there, :width] = other_ref[:, width:]
     p[there, width:] = other_ref[:, :width]
     own_ref[...] = p[:, :width]
+    left[...], right[...] = stacked(p[...], axis=1)
     for n in range(len(lists[0])):
         first = lists[0][n]
         second = lists[1][min(n, len(lists[1]) - 1)]
         i = jnp.where(core == 0, first[0], second[0])
         j = jnp.where(core == 0, first[1], second[1])
-        a = p[pl.ds(pl.multiple_of(i * TILE, TILE), TILE), :]
-        b = p[pl.ds(pl.multiple_of(j * TILE, TILE), TILE), :]
-        acc[n * TILE : (n + 1) * TILE, :] = dot(a, b, NT) * scale
+        a = left[pl.ds(pl.multiple_of(i * TILE, TILE), TILE), :]
+        b = right[pl.ds(pl.multiple_of(j * TILE, TILE), TILE), :]
+        acc[n * TILE : (n + 1) * TILE, :] = bf16_dot(a, b, NT) * scale
     size = acc.shape[0] // parts
     for k in range(parts):
         each = parts // len(outs)
@@ -398,7 +394,7 @@
     *pieces, predicted = call(
         functools.partial(gram_kernel, route, 1.0 / total),
         [f32(share // ways, TILE)] * ways + [f32(norb, width)],
-        [f32(norb, 2 * width), f32(share, TILE)],
+        [f32(norb, 2 * width), f32(share, TILE)] + [jax.ShapeDtypeStruct((norb, 12 * width), jnp.bfloat16)] * 2,
         [mine, other],
     )
     gram = direct_all_reduce(route, pieces, route.row_levels, levels)

time: 111 us -> 111 us (level)
  no operation moved by 1% of the time
where the time goes in v2:
time: 111 us
  starting transfers between devices  46.5 us (42%)
  waiting for transfers between devices  43.9 us (40%)
  Pallas kernels  18.5 us (17%)
  local copies, waits for them, and re-layouts  1.25 us (1%)
    ppermute x37, starting transfers between devices, swap(): return lax.ppermute(x, AXES, perm)  46.5 us
    ppermute x37, waiting for transfers between devices, swap(): return lax.ppermute(x, AXES, perm)  43.9 us
    pallas_call x9, Pallas kernels, call(): pl.pallas_call(kernel, cost_estimate=pl.CostEstimate(flops=flops, bytes_a...  18.4 us
  transfers between devices with their start and end apart: 37, of which 25 were waited for; matrix products, arithmetic and copies ran while one was open for 0% of the time, Pallas kernels for 3%

profile of v2, /device:TPU:0, one launch (start us, length us, event | category | flops | bytes accessed | tf_op | source)
XLA Modules:
  0.0 110.7 jit_solution(7015437659352598115)
XLA Ops:
  3.6 2.9 %collective-permute-start.17 = (f32[128,384]{1,0:T(8,128)S(1)}, f32[128,384]{1,0:T(8,128)S(1)}, u32[]{:S(2)}, u32[]{:S(2)}) collective-permute-start(f32[128,384]{1,0:T(8,128)S(1)} %get-tuple-element.23), channel_id=1, source_target_pairs={{0,8},{1,9},{2,10},{3,11},{4,20},{5,21},{6,22},{7,23},{8,0},{9,1},... | collective-permute-start | bytes 589832 | tf_op jit(solution)/shard_map/ppermute | solution.py:90
  6.5 3.6 %collective-permute-done.17 = f32[128,384]{1,0:T(8,128)S(1)} collective-permute-done((f32[128,384]{1,0:T(8,128)S(1)}, f32[128,384]{1,0:T(8,128)S(1)}, u32[]{:S(2)}, u32[]{:S(2)}) %collective-permute-start.17) | collective-permute-done | bytes 196640 | tf_op jit(solution)/shard_map/ppermute | solution.py:90
  10.2 2.1 %collective-permute-start.18 = (f32[64,384]{1,0:T(8,128)S(1)}, f32[64,384]{1,0:T(8,128)S(1)}, u32[]{:S(2)}, u32[]{:S(2)}) collective-permute-start(f32[64,384]{1,0:T(8,128)S(1)} %get-tuple-element.34), channel_id=1, source_target_pairs={{0,16},{1,17},{2,18},{3,19},{4,12},{5,13},{6,14},{7,15},{8,24},{9,... | collective-permute-start | bytes 294920 | tf_op jit(solution)/shard_map/ppermute | solution.py:90
  16.8 1.6 %collective-permute-start.19 = (f32[32,384]{1,0:T(8,128)S(1)}, f32[32,384]{1,0:T(8,128)S(1)}, u32[]{:S(2)}, u32[]{:S(2)}) collective-permute-start(f32[32,384]{1,0:T(8,128)S(1)} %get-tuple-element.40), channel_id=1, source_target_pairs={{0,1},{1,0},{2,3},{3,2},{4,5},{5,4},{6,7},{7,6},{8,9},{9,8},{10,11... | collective-permute-start | bytes 147464 | tf_op jit(solution)/shard_map/ppermute | solution.py:90
  20.9 2.6 %collective-permute-start.20 = (f32[16,384]{1,0:T(8,128)S(1)}, f32[16,384]{1,0:T(8,128)S(1)}, u32[]{:S(2)}, u32[]{:S(2)}) collective-permute-start(f32[16,384]{1,0:T(8,128)S(1)} %slice_add_fusion.16), channel_id=1, source_target_pairs={{0,2},{1,3},{2,0},{3,1},{4,6},{5,7},{6,4},{7,5},{8,10},{9,11},{10,... | collective-permute-start | bytes 73736 | tf_op jit(solution)/shard_map/ppermute | solution.py:90
  25.7 2.6 %collective-permute-start.21 = (f32[16,384]{1,0:T(8,128)S(1)}, f32[16,384]{1,0:T(8,128)S(1)}, u32[]{:S(2)}, u32[]{:S(2)}) collective-permute-start(f32[16,384]{1,0:T(8,128)S(1)} %fusion.2), channel_id=1, source_target_pairs={{0,2},{1,3},{2,0},{3,1},{4,6},{5,7},{6,4},{7,5},{8,10},{9,11},{10,... | collective-permute-start | bytes 73736 | tf_op jit(solution)/shard_map/ppermute | solution.py:90
  28.3 1.8 %collective-permute-start.11 = (f32[32,512]{1,0:T(8,128)S(1)}, f32[32,512]{1,0:T(8,128)S(1)}, u32[]{:S(2)}, u32[]{:S(2)}) collective-permute-start(f32[32,512]{1,0:T(8,128)S(1)} %get-tuple-element.36), channel_id=1, source_target_pairs={{0,1},{1,0},{2,3},{3,2},{4,5},{5,4},{6,7},{7,6},{8,9},{9,8},{10,11... | collective-permute-start | bytes 196616 | tf_op jit(solution)/shard_map/ppermute | solution.py:90
  32.3 2.7 %collective-permute-done.22 = f32[32,384]{1,0:T(8,128)S(1)} collective-permute-done((f32[32,384]{1,0:T(8,128)S(1)}, f32[32,384]{1,0:T(8,128)S(1)}, u32[]{:S(2)}, u32[]{:S(2)}) %collective-permute-start.22) | collective-permute-done | bytes 49184 | tf_op jit(solution)/shard_map/ppermute | solution.py:90
  36.2 2.5 %collective-permute-start.4 = (f32[16,512]{1,0:T(8,128)S(1)}, f32[16,512]{1,0:T(8,128)S(1)}, u32[]{:S(2)}, u32[]{:S(2)}) collective-permute-start(f32[16,512]{1,0:T(8,128)S(1)} %slice_add_fusion.14), channel_id=1, source_target_pairs={{0,2},{1,3},{2,0},{3,1},{4,6},{5,7},{6,4},{7,5},{8,10},{9,11},{10,... | collective-permute-start | bytes 98312 | tf_op jit(solution)/shard_map/ppermute | solution.py:90
  39.3 1.8 %collective-permute-done.4 = f32[16,512]{1,0:T(8,128)S(1)} collective-permute-done((f32[16,512]{1,0:T(8,128)S(1)}, f32[16,512]{1,0:T(8,128)S(1)}, u32[]{:S(2)}, u32[]{:S(2)}) %collective-permute-start.4) | collective-permute-done | bytes 32800 | tf_op jit(solution)/shard_map/ppermute | solution.py:90
  41.1 2.5 %collective-permute-start.5 = (f32[16,512]{1,0:T(8,128)S(1)}, f32[16,512]{1,0:T(8,128)S(1)}, u32[]{:S(2)}, u32[]{:S(2)}) collective-permute-start(f32[16,512]{1,0:T(8,128)S(1)} %fusion.1), channel_id=1, source_target_pairs={{0,2},{1,3},{2,0},{3,1},{4,6},{5,7},{6,4},{7,5},{8,10},{9,11},{10,... | collective-permute-start | bytes 98312 | tf_op jit(solution)/shard_map/ppermute | solution.py:90
  44.2 4.3 %collective-permute-done.13 = f32[16,512]{1,0:T(8,128)S(1)} collective-permute-done((f32[16,512]{1,0:T(8,128)S(1)}, f32[16,512]{1,0:T(8,128)S(1)}, u32[]{:S(2)}, u32[]{:S(2)}) %collective-permute-start.13) | collective-permute-done | bytes 32800 | tf_op jit(solution)/shard_map/ppermute | solution.py:90
  48.5 2.2 %collective-permute-start.14 = (f32[32,512]{1,0:T(8,128)S(1)}, f32[32,512]{1,0:T(8,128)S(1)}, u32[]{:S(2)}, u32[]{:S(2)}) collective-permute-start(f32[32,512]{1,0:T(8,128)S(1)} %pad_maximum_fusion.8), channel_id=1, source_target_pairs={{0,1},{1,0},{2,3},{3,2},{4,5},{5,4},{6,7},{7,6},{8,9},{9,8},{10,11... | collective-permute-start | bytes 196616 | tf_op jit(solution)/shard_map/ppermute | solution.py:90
  50.8 1.7 %collective-permute-start.24 = (f32[128,384]{1,0:T(8,128)S(1)}, f32[128,384]{1,0:T(8,128)S(1)}, u32[]{:S(2)}, u32[]{:S(2)}) collective-permute-start(f32[128,384]{1,0:T(8,128)S(1)} %pad_maximum_fusion.3), channel_id=1, source_target_pairs={{0,8},{1,9},{2,10},{3,11},{4,20},{5,21},{6,22},{7,23},{8,0},{9,1},... | collective-permute-start | bytes 589832 | tf_op jit(solution)/shard_map/ppermute | solution.py:90
  56.5 2.8 %collective-permute-done.15 = f32[64,512]{1,0:T(8,128)S(1)} collective-permute-done((f32[64,512]{1,0:T(8,128)S(1)}, f32[64,512]{1,0:T(8,128)S(1)}, u32[]{:S(2)}, u32[]{:S(2)}) %collective-permute-start.15) | collective-permute-done | bytes 131104 | tf_op jit(solution)/shard_map/ppermute | solution.py:90
  63.9 4.7 %collective-permute-done.8 = f32[128,512]{1,0:T(8,128)S(1)} collective-permute-done((f32[128,512]{1,0:T(8,128)S(1)}, f32[128,512]{1,0:T(8,128)S(1)}, u32[]{:S(2)}, u32[]{:S(2)}) %collective-permute-start.8) | collective-permute-done | bytes 262176 | tf_op jit(solution)/shard_map/ppermute | solution.py:90
  78.3 1.8 %collective-permute-done.29 = f32[160,128]{1,0:T(8,128)S(1)} collective-permute-done((f32[160,128]{1,0:T(8,128)S(1)}, f32[160,128]{1,0:T(8,128)S(1)}, u32[]{:S(2)}, u32[]{:S(2)}) %collective-permute-start.29) | collective-permute-done | bytes 81952 | tf_op jit(solution)/shard_map/ppermute | solution.py:90
  80.1 1.6 %collective-permute-start.32 = (f32[160,128]{1,0:T(8,128)S(1)}, f32[160,128]{1,0:T(8,128)S(1)}, u32[]{:S(2)}, u32[]{:S(2)}) collective-permute-start(f32[160,128]{1,0:T(8,128)S(1)} %add_add_fusion.1), channel_id=1, source_target_pairs={{0,3},{1,2},{2,1},{3,0},{4,7},{5,6},{6,5},{7,4},{8,11},{9,10},{10,... | collective-permute-start | bytes 245768 | tf_op jit(solution)/shard_map/ppermute | solution.py:90
  81.8 2.8 %collective-permute-start.30 = (f32[160,128]{1,0:T(8,128)S(1)}, f32[160,128]{1,0:T(8,128)S(1)}, u32[]{:S(2)}, u32[]{:S(2)}) collective-permute-start(f32[160,128]{1,0:T(8,128)S(1)} %add_add_fusion.1), channel_id=1, source_target_pairs={{0,2},{1,3},{2,0},{3,1},{4,6},{5,7},{6,4},{7,5},{8,10},{9,11},{10,... | collective-permute-start | bytes 245768 | tf_op jit(solution)/shard_map/ppermute | solution.py:90
  84.6 2.8 %collective-permute-done.32 = f32[160,128]{1,0:T(8,128)S(1)} collective-permute-done((f32[160,128]{1,0:T(8,128)S(1)}, f32[160,128]{1,0:T(8,128)S(1)}, u32[]{:S(2)}, u32[]{:S(2)}) %collective-permute-start.32) | collective-permute-done | bytes 81952 | tf_op jit(solution)/shard_map/ppermute | solution.py:90
  87.4 2.6 %collective-permute-done.30 = f32[160,128]{1,0:T(8,128)S(1)} collective-permute-done((f32[160,128]{1,0:T(8,128)S(1)}, f32[160,128]{1,0:T(8,128)S(1)}, u32[]{:S(2)}, u32[]{:S(2)}) %collective-permute-start.30) | collective-permute-done | bytes 81952 | tf_op jit(solution)/shard_map/ppermute | solution.py:90
  93.6 1.9 %collective-permute-done.35 = f32[160,128]{1,0:T(8,128)S(1)} collective-permute-done((f32[160,128]{1,0:T(8,128)S(1)}, f32[160,128]{1,0:T(8,128)S(1)}, u32[]{:S(2)}, u32[]{:S(2)}) %collective-permute-start.35) | collective-permute-done | bytes 81952 | tf_op jit(solution)/shard_map/ppermute | solution.py:90
  96.8 1.6 %collective-permute-done.36.other_ref = f32[640,128]{1,0:T(8,128)S(1)} collective-permute-done((f32[640,128]{1,0:T(8,128)S(1)}, f32[640,128]{1,0:T(8,128)S(1)}, u32[]{:S(2)}, u32[]{:S(2)}) %collective-permute-start.36) | collective-permute-done | bytes 327712 | tf_op jit(solution)/shard_map/ppermute | solution.py:90
  98.4 12.3 %shard_map.25 = f32[512,128]{1,0:T(8,128)} custom-call(f32[640,128]{1,0:T(8,128)S(1)} %pad_maximum_fusion.mine_ref, f32[640,128]{1,0:T(8,128)S(1)} %collective-permute-done.36.other_ref, f32[512,128]{1,0:T(8,128)S(1)} %get-tuple-element.28.p_ref), custom_call_target="tpu_custom_call" | custom-call | bytes 1179648 | tf_op jit(solution)/shard_map/pallas_call | solution.py:333
  (101 shorter events, 40.7 us)
Async XLA Ops:
  3.6 6.6 %collective-permute-start.17 = (f32[128,384]{1,0:T(8,128)S(1)}, f32[128,384]{1,0:T(8,128)S(1)}, u32[]{:S(2)}, u32[]{:S(2)}) collective-permute-start(f32[128,384]{1,0:T(8,128)S(1)} %get-tuple-element.23), channel_id=1, source_target_pairs={{0,8},{1,9},{2,10},{3,11},{4,20},{5,21},{6,22},{7,23},{8,0},{9,1},... | collective-permute-start | bytes 589832 | tf_op jit(solution)/shard_map/ppermute | solution.py:90
  10.2 6.6 %collective-permute-start.18 = (f32[64,384]{1,0:T(8,128)S(1)}, f32[64,384]{1,0:T(8,128)S(1)}, u32[]{:S(2)}, u32[]{:S(2)}) collective-permute-start(f32[64,384]{1,0:T(8,128)S(1)} %get-tuple-element.34), channel_id=1, source_target_pairs={{0,16},{1,17},{2,18},{3,19},{4,12},{5,13},{6,14},{7,15},{8,24},{9,... | collective-permute-start | bytes 294920 | tf_op jit(solution)/shard_map/ppermute | solution.py:90
  13.4 6.4 %collective-permute-start.9 = (f32[128,512]{1,0:T(8,128)S(1)}, f32[128,512]{1,0:T(8,128)S(1)}, u32[]{:S(2)}, u32[]{:S(2)}) collective-permute-start(f32[128,512]{1,0:T(8,128)S(1)} %get-tuple-element.21), channel_id=1, source_target_pairs={{0,8},{1,9},{2,10},{3,11},{4,20},{5,21},{6,22},{7,23},{8,0},{9,1},... | collective-permute-start | bytes 786440 | tf_op jit(solution)/shard_map/ppermute | solution.py:90
  16.1 7.9 %collective-permute-start.1 = (f32[128,512]{1,0:T(8,128)S(1)}, f32[128,512]{1,0:T(8,128)S(1)}, u32[]{:S(2)}, u32[]{:S(2)}) collective-permute-start(f32[128,512]{1,0:T(8,128)S(1)} %get-tuple-element.19), channel_id=1, source_target_pairs={{0,8},{1,9},{2,10},{3,11},{4,20},{5,21},{6,22},{7,23},{8,0},{9,1},... | collective-permute-start | bytes 786440 | tf_op jit(solution)/shard_map/ppermute | solution.py:90
  19.9 8.4 %collective-permute-start.10 = (f32[64,512]{1,0:T(8,128)S(1)}, f32[64,512]{1,0:T(8,128)S(1)}, u32[]{:S(2)}, u32[]{:S(2)}) collective-permute-start(f32[64,512]{1,0:T(8,128)S(1)} %get-tuple-element.30), channel_id=1, source_target_pairs={{0,16},{1,17},{2,18},{3,19},{4,12},{5,13},{6,14},{7,15},{8,24},{9,... | collective-permute-start | bytes 393224 | tf_op jit(solution)/shard_map/ppermute | solution.py:90
  24.1 5.9 %collective-permute-start.2 = (f32[64,512]{1,0:T(8,128)S(1)}, f32[64,512]{1,0:T(8,128)S(1)}, u32[]{:S(2)}, u32[]{:S(2)}) collective-permute-start(f32[64,512]{1,0:T(8,128)S(1)} %get-tuple-element.32), channel_id=1, source_target_pairs={{0,16},{1,17},{2,18},{3,19},{4,12},{5,13},{6,14},{7,15},{8,24},{9,... | collective-permute-start | bytes 393224 | tf_op jit(solution)/shard_map/ppermute | solution.py:90
  25.7 5.2 %collective-permute-start.21 = (f32[16,384]{1,0:T(8,128)S(1)}, f32[16,384]{1,0:T(8,128)S(1)}, u32[]{:S(2)}, u32[]{:S(2)}) collective-permute-start(f32[16,384]{1,0:T(8,128)S(1)} %fusion.2), channel_id=1, source_target_pairs={{0,2},{1,3},{2,0},{3,1},{4,6},{5,7},{6,4},{7,5},{8,10},{9,11},{10,... | collective-permute-start | bytes 73736 | tf_op jit(solution)/shard_map/ppermute | solution.py:90
  28.3 10.4 %collective-permute-start.11 = (f32[32,512]{1,0:T(8,128)S(1)}, f32[32,512]{1,0:T(8,128)S(1)}, u32[]{:S(2)}, u32[]{:S(2)}) collective-permute-start(f32[32,512]{1,0:T(8,128)S(1)} %get-tuple-element.36), channel_id=1, source_target_pairs={{0,1},{1,0},{2,3},{3,2},{4,5},{5,4},{6,7},{7,6},{8,9},{9,8},{10,11... | collective-permute-start | bytes 196616 | tf_op jit(solution)/shard_map/ppermute | solution.py:90
  30.1 6.1 %collective-permute-start.3 = (f32[32,512]{1,0:T(8,128)S(1)}, f32[32,512]{1,0:T(8,128)S(1)}, u32[]{:S(2)}, u32[]{:S(2)}) collective-permute-start(f32[32,512]{1,0:T(8,128)S(1)} %get-tuple-element.38), channel_id=1, source_target_pairs={{0,1},{1,0},{2,3},{3,2},{4,5},{5,4},{6,7},{7,6},{8,9},{9,8},{10,11... | collective-permute-start | bytes 196616 | tf_op jit(solution)/shard_map/ppermute | solution.py:90
  35.0 15.8 %collective-permute-start.23 = (f32[64,384]{1,0:T(8,128)S(1)}, f32[64,384]{1,0:T(8,128)S(1)}, u32[]{:S(2)}, u32[]{:S(2)}) collective-permute-start(f32[64,384]{1,0:T(8,128)S(1)} %pad_maximum_fusion.6), channel_id=1, source_target_pairs={{0,16},{1,17},{2,18},{3,19},{4,12},{5,13},{6,14},{7,15},{8,24},{9,... | collective-permute-start | bytes 294920 | tf_op jit(solution)/shard_map/ppermute | solution.py:90
  38.7 4.9 %collective-permute-start.12 = (f32[16,512]{1,0:T(8,128)S(1)}, f32[16,512]{1,0:T(8,128)S(1)}, u32[]{:S(2)}, u32[]{:S(2)}) collective-permute-start(f32[16,512]{1,0:T(8,128)S(1)} %slice_add_fusion.12), channel_id=1, source_target_pairs={{0,2},{1,3},{2,0},{3,1},{4,6},{5,7},{6,4},{7,5},{8,10},{9,11},{10,... | collective-permute-start | bytes 98312 | tf_op jit(solution)/shard_map/ppermute | solution.py:90
  41.1 9.5 %collective-permute-start.5 = (f32[16,512]{1,0:T(8,128)S(1)}, f32[16,512]{1,0:T(8,128)S(1)}, u32[]{:S(2)}, u32[]{:S(2)}) collective-permute-start(f32[16,512]{1,0:T(8,128)S(1)} %fusion.1), channel_id=1, source_target_pairs={{0,2},{1,3},{2,0},{3,1},{4,6},{5,7},{6,4},{7,5},{8,10},{9,11},{10,... | collective-permute-start | bytes 98312 | tf_op jit(solution)/shard_map/ppermute | solution.py:90
  50.8 11.0 %collective-permute-start.24 = (f32[128,384]{1,0:T(8,128)S(1)}, f32[128,384]{1,0:T(8,128)S(1)}, u32[]{:S(2)}, u32[]{:S(2)}) collective-permute-start(f32[128,384]{1,0:T(8,128)S(1)} %pad_maximum_fusion.3), channel_id=1, source_target_pairs={{0,8},{1,9},{2,10},{3,11},{4,20},{5,21},{6,22},{7,23},{8,0},{9,1},... | collective-permute-start | bytes 589832 | tf_op jit(solution)/shard_map/ppermute | solution.py:90
  52.9 6.4 %collective-permute-start.15 = (f32[64,512]{1,0:T(8,128)S(1)}, f32[64,512]{1,0:T(8,128)S(1)}, u32[]{:S(2)}, u32[]{:S(2)}) collective-permute-start(f32[64,512]{1,0:T(8,128)S(1)} %pad_maximum_fusion.5), channel_id=1, source_target_pairs={{0,16},{1,17},{2,18},{3,19},{4,12},{5,13},{6,14},{7,15},{8,24},{9,... | collective-permute-start | bytes 393224 | tf_op jit(solution)/shard_map/ppermute | solution.py:90
  55.0 6.1 %collective-permute-start.7 = (f32[64,512]{1,0:T(8,128)S(1)}, f32[64,512]{1,0:T(8,128)S(1)}, u32[]{:S(2)}, u32[]{:S(2)}) collective-permute-start(f32[64,512]{1,0:T(8,128)S(1)} %pad_maximum_fusion.4), channel_id=1, source_target_pairs={{0,16},{1,17},{2,18},{3,19},{4,12},{5,13},{6,14},{7,15},{8,24},{9,... | collective-permute-start | bytes 393224 | tf_op jit(solution)/shard_map/ppermute | solution.py:90
  59.3 9.3 %collective-permute-start.16 = (f32[128,512]{1,0:T(8,128)S(1)}, f32[128,512]{1,0:T(8,128)S(1)}, u32[]{:S(2)}, u32[]{:S(2)}) collective-permute-start(f32[128,512]{1,0:T(8,128)S(1)} %pad_maximum_fusion.2), channel_id=1, source_target_pairs={{0,8},{1,9},{2,10},{3,11},{4,20},{5,21},{6,22},{7,23},{8,0},{9,1},... | collective-permute-start | bytes 786440 | tf_op jit(solution)/shard_map/ppermute | solution.py:90
  61.1 7.5 %collective-permute-start.8 = (f32[128,512]{1,0:T(8,128)S(1)}, f32[128,512]{1,0:T(8,128)S(1)}, u32[]{:S(2)}, u32[]{:S(2)}) collective-permute-start(f32[128,512]{1,0:T(8,128)S(1)} %pad_maximum_fusion.1), channel_id=1, source_target_pairs={{0,8},{1,9},{2,10},{3,11},{4,20},{5,21},{6,22},{7,23},{8,0},{9,1},... | collective-permute-start | bytes 786440 | tf_op jit(solution)/shard_map/ppermute | solution.py:90
  72.4 5.0 %collective-permute-start.27 = (f32[160,128]{1,0:T(8,128)S(1)}, f32[160,128]{1,0:T(8,128)S(1)}, u32[]{:S(2)}, u32[]{:S(2)}) collective-permute-start(f32[160,128]{1,0:T(8,128)S(1)} %get-tuple-element.25), channel_id=1, source_target_pairs={{0,16},{1,17},{2,18},{3,19},{4,12},{5,13},{6,14},{7,15},{8,24},{9,... | collective-permute-start | bytes 245768 | tf_op jit(solution)/shard_map/ppermute | solution.py:90
  73.1 5.2 %collective-permute-start.28 = (f32[160,128]{1,0:T(8,128)S(1)}, f32[160,128]{1,0:T(8,128)S(1)}, u32[]{:S(2)}, u32[]{:S(2)}) collective-permute-start(f32[160,128]{1,0:T(8,128)S(1)} %get-tuple-element.26), channel_id=1, source_target_pairs={{0,8},{1,9},{2,10},{3,11},{4,20},{5,21},{6,22},{7,23},{8,0},{9,1},... | collective-permute-start | bytes 245768 | tf_op jit(solution)/shard_map/ppermute | solution.py:90
  74.4 5.7 %collective-permute-start.29 = (f32[160,128]{1,0:T(8,128)S(1)}, f32[160,128]{1,0:T(8,128)S(1)}, u32[]{:S(2)}, u32[]{:S(2)}) collective-permute-start(f32[160,128]{1,0:T(8,128)S(1)} %get-tuple-element.27), channel_id=1, source_target_pairs={{0,24},{1,25},{2,26},{3,27},{4,28},{5,29},{6,30},{7,31},{8,16},{9,... | collective-permute-start | bytes 245768 | tf_op jit(solution)/shard_map/ppermute | solution.py:90
  80.1 7.3 %collective-permute-start.32 = (f32[160,128]{1,0:T(8,128)S(1)}, f32[160,128]{1,0:T(8,128)S(1)}, u32[]{:S(2)}, u32[]{:S(2)}) collective-permute-start(f32[160,128]{1,0:T(8,128)S(1)} %add_add_fusion.1), channel_id=1, source_target_pairs={{0,3},{1,2},{2,1},{3,0},{4,7},{5,6},{6,5},{7,4},{8,11},{9,10},{10,... | collective-permute-start | bytes 245768 | tf_op jit(solution)/shard_map/ppermute | solution.py:90
  81.8 5.6 %collective-permute-start.31 = (f32[160,128]{1,0:T(8,128)S(1)}, f32[160,128]{1,0:T(8,128)S(1)}, u32[]{:S(2)}, u32[]{:S(2)}) collective-permute-start(f32[160,128]{1,0:T(8,128)S(1)} %add_add_fusion.1), channel_id=1, source_target_pairs={{0,1},{1,0},{2,3},{3,2},{4,5},{5,4},{6,7},{7,6},{8,9},{9,8},{10,11... | collective-permute-start | bytes 245768 | tf_op jit(solution)/shard_map/ppermute | solution.py:90
  81.8 8.2 %collective-permute-start.30 = (f32[160,128]{1,0:T(8,128)S(1)}, f32[160,128]{1,0:T(8,128)S(1)}, u32[]{:S(2)}, u32[]{:S(2)}) collective-permute-start(f32[160,128]{1,0:T(8,128)S(1)} %add_add_fusion.1), channel_id=1, source_target_pairs={{0,2},{1,3},{2,0},{3,1},{4,6},{5,7},{6,4},{7,5},{8,10},{9,11},{10,... | collective-permute-start | bytes 245768 | tf_op jit(solution)/shard_map/ppermute | solution.py:90
  90.0 5.4 %collective-permute-start.35 = (f32[160,128]{1,0:T(8,128)S(1)}, f32[160,128]{1,0:T(8,128)S(1)}, u32[]{:S(2)}, u32[]{:S(2)}) collective-permute-start(f32[160,128]{1,0:T(8,128)S(1)} %add_add_fusion), channel_id=1, source_target_pairs={{0,24},{1,25},{2,26},{3,27},{4,28},{5,29},{6,30},{7,31},{8,16},{9,... | collective-permute-start | bytes 245768 | tf_op jit(solution)/shard_map/ppermute | solution.py:90
  (14 other events, 49.2 us)
